TPU v7x, 8 devices: a whole 2x2x1 slice. The times are simulated.
8 devices in a mesh: dp: 4 (over z, y, x), emb: 2 (over core).
Axes of the slice: x: 2, y: 2, z: 1, core: 2. Of those that a mesh axis runs over, the one named last changes fastest.
Arguments:
- tok_ids: int32 [8192], P(('dp', 'emb'))
- resid_in: bfloat16 [8192, 896], P(('dp', 'emb'))
- cot_out: bfloat16 [8192, 896], P(('dp', 'emb'))
- tables: bfloat16 [6, 151936, 128], P(None, 'emb')
- w_up: bfloat16 [6, 896, 4864], replicated
- w_down: bfloat16 [6, 4864, 896], replicated
- w_gate: bfloat16 [6, 896, 128], replicated
- w_proj: bfloat16 [6, 128, 896], replicated
Outputs:
- output 1: bfloat16 [8192, 896], P(('dp', 'emb'))
- output 2: float32 [6, 151936, 128], P(None, 'emb')
All inputs are finite; a program needn't handle non-finite values.
Results may differ from a plain program's by a relative error of at most 0.0149798.
Values are sent between devices in bfloat16 or wider.
A program may use at most 1.75 GiB of HBM per device.

v0:
```python
import jax
import jax.numpy as jnp
from jax import lax
from jax.sharding import PartitionSpec as P

NORM_EPS = 1e-6


def rms_norm(x_f32):
    return x_f32 * lax.rsqrt(jnp.mean(x_f32 * x_f32, axis=-1, keepdims=True) + NORM_EPS)


def layer_forward(resid_cur, fetched, w_up_l, w_down_l, w_gate_l, w_proj_l):
    x_f32 = resid_cur.astype(jnp.float32)
    normed = rms_norm(x_f32).astype(jnp.bfloat16)
    up_pre = jnp.dot(normed, w_up_l, preferred_element_type=jnp.float32)
    hidden = jax.nn.gelu(up_pre).astype(jnp.bfloat16)
    mlp_out = jnp.dot(hidden, w_down_l, preferred_element_type=jnp.float32)
    gate_pre = jnp.dot(normed, w_gate_l, preferred_element_type=jnp.float32)
    gate_act = jax.nn.gelu(gate_pre)
    mixed_in = (gate_act * fetched.astype(jnp.float32)).astype(jnp.bfloat16)
    proj_out = jnp.dot(mixed_in, w_proj_l, preferred_element_type=jnp.float32)
    resid_next = (x_f32 + mlp_out + proj_out).astype(jnp.bfloat16)
    return resid_next, (resid_cur, up_pre, gate_pre, gate_act, fetched)


def layer_backward(cot_next, layer_saved, w_up_l, w_down_l, w_gate_l, w_proj_l):
    resid_cur, up_pre, gate_pre, gate_act, fetched = layer_saved
    d_mixed = jnp.einsum('td,ed->te', cot_next, w_proj_l, preferred_element_type=jnp.float32).astype(jnp.bfloat16).astype(jnp.float32)
    grad_rows = gate_act * d_mixed
    d_gate_act = d_mixed * fetched.astype(jnp.float32)
    d_gate_pre = jax.vjp(jax.nn.gelu, gate_pre)[1](d_gate_act)[0]
    d_hidden = jnp.einsum('td,fd->tf', cot_next, w_down_l, preferred_element_type=jnp.float32).astype(jnp.bfloat16)
    d_up_pre = jax.vjp(jax.nn.gelu, up_pre)[1](d_hidden.astype(jnp.float32))[0]
    d_norm_mlp = jnp.einsum('tf,df->td', d_up_pre.astype(jnp.bfloat16), w_up_l, preferred_element_type=jnp.float32).astype(jnp.bfloat16)
    d_norm_gate = jnp.einsum('te,de->td', d_gate_pre.astype(jnp.bfloat16), w_gate_l, preferred_element_type=jnp.float32).astype(jnp.bfloat16)
    d_normed = (d_norm_mlp + d_norm_gate).astype(jnp.float32)
    d_x_norm = jax.vjp(rms_norm, resid_cur.astype(jnp.float32))[1](d_normed)[0]
    cot_cur = (cot_next.astype(jnp.float32) + d_x_norm).astype(jnp.bfloat16)
    return cot_cur, grad_rows


def route_plan(tok_ids, range_rows, n_emb, cap_rows):
    owner_ids = tok_ids // range_rows
    local_off = tok_ids - owner_ids * range_rows
    one_hot = (owner_ids[:, None] == jnp.arange(n_emb, dtype=jnp.int32)[None, :]).astype(jnp.int32)
    rank_in = jnp.sum((jnp.cumsum(one_hot, axis=0) - one_hot) * one_hot, axis=1)
    slot_of = owner_ids * cap_rows + rank_in
    tok_count = tok_ids.shape[0]
    slot_token = jnp.zeros((n_emb * cap_rows,), jnp.int32).at[slot_of].set(jnp.arange(tok_count, dtype=jnp.int32))
    slot_mask = jnp.zeros((n_emb * cap_rows,), jnp.float32).at[slot_of].set(1.0)
    send_ids = jnp.where(slot_mask > 0, jnp.take(local_off, slot_token), 0)
    return slot_of, slot_token, slot_mask, send_ids


def solution(mesh):
    n_emb = mesh.shape['emb']
    tok_spec = P(('dp', 'emb'))
    act_spec = P(('dp', 'emb'), None)
    table_spec = P(None, 'emb', None)
    full_spec = P(None, None, None)

    def device_body(tok_ids, resid_in, cot_out, tables, w_up, w_down, w_gate, w_proj):
        n_layers = tables.shape[0]
        range_rows = tables.shape[1]
        tok_count = tok_ids.shape[0]
        cap_rows = min(2 * tok_count // n_emb, 3 * tok_count // 4)
        slot_of, slot_token, slot_mask, send_ids = route_plan(tok_ids, range_rows, n_emb, cap_rows)
        recv_ids = lax.all_to_all(send_ids, 'emb', 0, 0, tiled=True)
        resid_cur = resid_in
        saved_acts = []
        for l_idx in range(n_layers):
            served = jnp.take(tables[l_idx], recv_ids, axis=0)
            returned = lax.all_to_all(served, 'emb', 0, 0, tiled=True)
            fetched = jnp.take(returned, slot_of, axis=0)
            resid_cur, layer_saved = layer_forward(resid_cur, fetched, w_up[l_idx], w_down[l_idx], w_gate[l_idx], w_proj[l_idx])
            saved_acts.append(layer_saved)
        cot_cur = cot_out
        grad_list = [None] * n_layers
        for l_idx in reversed(range(n_layers)):
            cot_cur, grad_rows = layer_backward(cot_cur, saved_acts[l_idx], w_up[l_idx], w_down[l_idx], w_gate[l_idx], w_proj[l_idx])
            outgoing = jnp.take(grad_rows, slot_token, axis=0) * slot_mask[:, None]
            incoming = lax.all_to_all(outgoing, 'emb', 0, 0, tiled=True)
            shard_grad = jax.ops.segment_sum(incoming, recv_ids, num_segments=range_rows)
            grad_list[l_idx] = lax.psum(shard_grad, 'dp')
        return resid_cur, jnp.stack(grad_list)

    return jax.shard_map(device_body, mesh=mesh, in_specs=(tok_spec, act_spec, act_spec, table_spec, full_spec, full_spec, full_spec, full_spec), out_specs=(act_spec, table_spec), check_vma=False)
```

profile of v0, /device:TPU:0, one launch (start us, length us, event | category | flops | bytes accessed | tf_op | source)
XLA Modules:
  0.0 4693.1 jit_solution(8341946584132823914)
XLA Ops:
  9.7 4.3 scatter_custom_fusion.1
  14.0 5.9 gather_fusion
  29.2 75.3 %slice_bitcast_fusion = (bf16[75968,128]{1,0:T(8,128)(2,1)}, bf16[75968,128]{1,0:T(8,128)(2,1)}, bf16[75968,128]{1,0:T(8,128)(2,1)}, bf16[75968,128]{1,0:T(8,128...) fusion(bf16[6,75968,128]{2,1,0:T(8,128)(2,1)} %param.17), kind=kLoop, calls=%fused_computation.123 | loop fusion | bytes 233373696 | tf_op jit(solution)/shard_map/squeeze | solution.py:73
  104.5 11.7 gather_fusion.11
  116.1 11.7 gather_fusion.3
  127.8 11.9 gather_fusion.5
  139.7 11.7 gather_fusion.7
  151.4 11.7 gather_fusion.9
  163.0 11.7 gather_fusion.1
  185.4 17.6 fusion.128
  211.6 21.7 fusion.171
  235.3 17.7 fusion.125
  260.7 21.9 fusion.176
  284.7 17.5 fusion.119
  310.1 21.9 fusion.181
  333.9 17.5 fusion.113
  359.1 21.9 fusion.186
  383.0 17.5 fusion.107
  408.1 21.9 fusion.191
  432.0 17.5 fusion.101
  458.1 24.1 fusion.611
  482.2 14.5 fusion.93
  500.0 25.4 fusion.607
  526.9 14.5 fusion.89
  544.7 25.4 fusion.603
  570.9 14.5 fusion.85
  588.7 25.6 fusion.599
  614.9 14.5 fusion.81
  634.4 25.2 fusion.595
  678.1 14.7 fusion.77
  704.9 5.0 all_to_all.158
  713.4 25.4 scatter_custom_fusion.2
  738.8 4.3 all-to-all-start.9
  743.2 24.1 scatter_custom_fusion.3
  767.4 24.5 scatter_custom_fusion.4
  791.9 9.1 all_to_all.159
  804.6 24.1 scatter_custom_fusion.5
  832.6 24.1 scatter_custom_fusion.6
  856.7 24.4 scatter_custom_fusion.7
  883.0 21.8 fusion.194
  907.3 1793.7 %all-reduce.5.cloned.1.call-done = (f32[1,75968,128]{2,1,0:T(8,128)}, f32[1,75968,128]{2,1,0:T(8,128)}, f32[1,75968,128]{2,1,0:T(8,128)}) async-done(((f32[1,75968,128]{2,1,0:T(8,128)}, f32[1,75968,128]{2,1,0:T(8,128)}, f32[1,75968,128]{2,1,0:T(8,128)}), (f32[1,75968,128]{2,1,0:T(8,128)}, f32[1,75968,128]{2,1,0:T(8,128)}, f32[1,75968,128]{2,1,0:T(8,128)})) %all-reduce.5.cloned.1.call-update) | async-done | bytes 116686864 | tf_op jit(solution)/shard_map/psum | solution.py:85
  2701.0 31.1 constant_dynamic-update-slice_fusion.5
  2732.2 30.6 constant_dynamic-update-slice_fusion.4
  2762.9 12.9 constant_dynamic-update-slice_fusion.3
  2775.8 1835.3 %all-reduce.7.cloned.1.call-done = (f32[1,75968,128]{2,1,0:T(8,128)}, f32[1,75968,128]{2,1,0:T(8,128)}, f32[1,75968,128]{2,1,0:T(8,128)}) async-done(((f32[1,75968,128]{2,1,0:T(8,128)}, f32[1,75968,128]{2,1,0:T(8,128)}, f32[1,75968,128]{2,1,0:T(8,128)}), (f32[1,75968,128]{2,1,0:T(8,128)}, f32[1,75968,128]{2,1,0:T(8,128)}, f32[1,75968,128]{2,1,0:T(8,128)})) %all-reduce.7.cloned.1.call-update) | async-done | bytes 116686864 | tf_op jit(solution)/shard_map/psum | solution.py:85
  4611.1 31.1 constant_dynamic-update-slice_fusion.2
  4642.3 30.6 constant_dynamic-update-slice_fusion.1
  4673.0 12.9 constant_dynamic-update-slice_fusion
  (273 shorter events, 143.3 us)
Async XLA Ops:
  14.0 90.4 %copy-start.40 = (s32[2048]{0:T(1024)}, s32[2048]{0:T(1024)S(1)}, u32[]{:S(2)}) copy-start(s32[2048]{0:T(1024)S(1)} %pad_clamp_fusion.1) | copy-start | bytes 24580
  24.2 80.2 %copy-start.43 = (f32[1536]{0:T(1024)}, f32[1536]{0:T(1024)S(1)}, u32[]{:S(2)}) copy-start(f32[1536]{0:T(1024)S(1)} %scatter_custom_fusion) | copy-start | bytes 18436
  29.1 75.3 %copy-start.42 = (s32[1536]{0:T(1024)}, s32[1536]{0:T(1024)S(1)}, u32[]{:S(2)}) copy-start(s32[1536]{0:T(1024)S(1)} %all_to_all.106) | copy-start | bytes 18436
  176.4 26.6 all-to-all-start.1
  185.4 24.5 copy-start.37
  203.0 50.0 %all-to-all-start.2 = ((bf16[2,768,128]{2,1,0:T(8,128)(2,1)}), bf16[2,768,128]{2,1,0:T(8,128)(2,1)S(1)}, u32[]{:S(2)}, u32[]{:S(2)}) async-start(bf16[2,768,128]{2,1,0:T(8,128)(2,1)} %bitcast.13), calls=%async_computation.2 | async-start | bytes 786432 | tf_op jit(solution)/shard_map/all_to_all | solution.py:74
  235.3 24.6 copy-start.10
  235.3 24.6 copy-start.6
  253.0 49.1 %all-to-all-start.3 = ((bf16[2,768,128]{2,1,0:T(8,128)(2,1)}), bf16[2,768,128]{2,1,0:T(8,128)(2,1)S(1)}, u32[]{:S(2)}, u32[]{:S(2)}) async-start(bf16[2,768,128]{2,1,0:T(8,128)(2,1)} %bitcast.20), calls=%async_computation.3 | async-start | bytes 786432 | tf_op jit(solution)/shard_map/all_to_all | solution.py:74
  284.7 24.6 copy-start.13
  302.1 49.3 %all-to-all-start.4 = ((bf16[2,768,128]{2,1,0:T(8,128)(2,1)}), bf16[2,768,128]{2,1,0:T(8,128)(2,1)S(1)}, u32[]{:S(2)}, u32[]{:S(2)}) async-start(bf16[2,768,128]{2,1,0:T(8,128)(2,1)} %bitcast.27), calls=%async_computation.4 | async-start | bytes 786432 | tf_op jit(solution)/shard_map/all_to_all | solution.py:74
  351.4 49.0 %all-to-all-start.5 = ((bf16[2,768,128]{2,1,0:T(8,128)(2,1)}), bf16[2,768,128]{2,1,0:T(8,128)(2,1)S(1)}, u32[]{:S(2)}, u32[]{:S(2)}) async-start(bf16[2,768,128]{2,1,0:T(8,128)(2,1)} %bitcast.34), calls=%async_computation.5 | async-start | bytes 786432 | tf_op jit(solution)/shard_map/all_to_all | solution.py:74
  400.4 49.1 %all-to-all-start.6 = ((bf16[2,768,128]{2,1,0:T(8,128)(2,1)}), bf16[2,768,128]{2,1,0:T(8,128)(2,1)S(1)}, u32[]{:S(2)}, u32[]{:S(2)}) async-start(bf16[2,768,128]{2,1,0:T(8,128)(2,1)} %bitcast.41), calls=%async_computation.6 | async-start | bytes 786432 | tf_op jit(solution)/shard_map/all_to_all | solution.py:74
  432.0 64.7 %copy-start.8 = (f32[1024,128]{1,0:T(8,128)}, f32[1024,128]{1,0:T(8,128)S(1)}, u32[]{:S(2)}) copy-start(f32[1024,128]{1,0:T(8,128)S(1)} %fusion.212) | copy-start | bytes 1572868
  452.7 43.9 copy-start.27
  500.0 25.5 copy-start.7
  500.0 25.5 copy-start.18
  544.7 25.4 copy-start.16
  588.7 25.6 copy-start.14
  632.9 26.8 copy-start.3
  634.4 25.2 copy-start
  634.4 25.2 copy-start.41
  709.9 28.9 all-to-all-start.8
  738.8 28.5 all-to-all-start.9
  743.2 1957.8 %all-reduce.5.cloned.1.call-start = ((), (), s32[]{:S(2)}) async-start(), calls=%async_computation.13 | async-start | bytes 233373696 | tf_op jit(solution)/shard_map/psum | solution.py:85
  801.1 27.7 all-to-all-start.11
  828.8 27.9 all-to-all-start.12
  832.3 3778.8 %all-reduce.7.cloned.1.call-start = ((), (), s32[]{:S(2)}) async-start(), calls=%async_computation.14 | async-start | bytes 233373696 | tf_op jit(solution)/shard_map/psum | solution.py:85
  2701.0 61.8 %slice-start = ((s8[38895616]{0:T(1024)(128)(4,1)}), s8[4194304]{0:T(1024)(128)(4,1)S(1)}, s32[]{:S(2)}) async-start(s8[38895616]{0:T(1024)(128)(4,1)} %bitcast.300), calls=%async_computation.15 | async-start | bytes 8388608
  2701.0 61.8 %slice-start.1 = ((s8[38895616]{0:T(1024)(128)(4,1)}), s8[4194304]{0:T(1024)(128)(4,1)S(1)}, s32[]{:S(2)}) async-start(s8[38895616]{0:T(1024)(128)(4,1)} %bitcast.300), calls=%async_computation.16 | async-start | bytes 8388608
  2701.0 61.8 %slice-start.2 = ((s8[38895616]{0:T(1024)(128)(4,1)}), s8[4194304]{0:T(1024)(128)(4,1)S(1)}, s32[]{:S(2)}) async-start(s8[38895616]{0:T(1024)(128)(4,1)} %bitcast.300), calls=%async_computation.17 | async-start | bytes 8388608
  2701.0 61.8 %slice-start.3 = ((s8[38895616]{0:T(1024)(128)(4,1)}), s8[4194304]{0:T(1024)(128)(4,1)S(1)}, s32[]{:S(2)}) async-start(s8[38895616]{0:T(1024)(128)(4,1)} %bitcast.300), calls=%async_computation.18 | async-start | bytes 8388608
  2701.0 61.8 %slice-start.4 = ((s8[38895616]{0:T(1024)(128)(4,1)}), s8[4194304]{0:T(1024)(128)(4,1)S(1)}, s32[]{:S(2)}) async-start(s8[38895616]{0:T(1024)(128)(4,1)} %bitcast.300), calls=%async_computation.19 | async-start | bytes 8388608
  2732.1 30.7 slice-start.5
  2732.1 30.7 slice-start.6
  2732.1 30.7 slice-start.7
  2732.1 30.7 slice-start.8
  2732.1 30.7 slice-start.9
  4611.1 61.8 %slice-start.10 = ((s8[38895616]{0:T(1024)(128)(4,1)}), s8[4194304]{0:T(1024)(128)(4,1)S(1)}, s32[]{:S(2)}) async-start(s8[38895616]{0:T(1024)(128)(4,1)} %bitcast.302), calls=%async_computation.25 | async-start | bytes 8388608
  4611.1 61.8 %slice-start.11 = ((s8[38895616]{0:T(1024)(128)(4,1)}), s8[4194304]{0:T(1024)(128)(4,1)S(1)}, s32[]{:S(2)}) async-start(s8[38895616]{0:T(1024)(128)(4,1)} %bitcast.302), calls=%async_computation.26 | async-start | bytes 8388608
  4611.1 61.8 %slice-start.12 = ((s8[38895616]{0:T(1024)(128)(4,1)}), s8[4194304]{0:T(1024)(128)(4,1)S(1)}, s32[]{:S(2)}) async-start(s8[38895616]{0:T(1024)(128)(4,1)} %bitcast.302), calls=%async_computation.27 | async-start | bytes 8388608
  4611.1 61.8 %slice-start.13 = ((s8[38895616]{0:T(1024)(128)(4,1)}), s8[4194304]{0:T(1024)(128)(4,1)S(1)}, s32[]{:S(2)}) async-start(s8[38895616]{0:T(1024)(128)(4,1)} %bitcast.302), calls=%async_computation.28 | async-start | bytes 8388608
  4611.1 61.8 %slice-start.14 = ((s8[38895616]{0:T(1024)(128)(4,1)}), s8[4194304]{0:T(1024)(128)(4,1)S(1)}, s32[]{:S(2)}) async-start(s8[38895616]{0:T(1024)(128)(4,1)} %bitcast.302), calls=%async_computation.29 | async-start | bytes 8388608
  4642.3 30.7 slice-start.15
  4642.3 30.7 slice-start.16
  4642.3 30.7 slice-start.17
  4642.3 30.7 slice-start.18
  4642.3 30.7 slice-start.19
  (49 other events, 720.4 us)
Sparse Core Ops, SparseCore 0:
  792.0 1908.8 all-reduce.4
  2704.9 1906.1 all-reduce.6
where the time goes:
time: 4700 us; the launch traced here: 4690 us
  waiting for transfers between devices  3630 us (77%)
  matrix products  470 us (10%)
  local copies, waits for them, and re-layouts  362 us (8%)
  other arithmetic  161 us (3%)
    psum x2, waiting for transfers between devices, device_body(): grad_list[l_idx] = lax.psum(shard_grad, 'dp')  3630 us
    scatter-add x6, other arithmetic, device_body(): jax.ops.segment_sum(incoming, recv_ids, num_segments=range_rows)  147 us
    unnamed x178, local copies, waits for them, and re-layouts  147 us
    dot_general x6, matrix products, layer_forward(): mlp_out = jnp.dot(hidden, w_down_l, preferred_element_type=jnp.float32)  131 us
    dot_general x5, matrix products, layer_backward(): jnp.einsum('td,fd->tf', cot_next, w_down_l, preferred_element_type=jnp.fl...  126 us
    dot_general x6, matrix products, layer_forward(): up_pre = jnp.dot(normed, w_up_l, preferred_element_type=jnp.float32)  105 us
  transfers between devices with their start and end apart: 12, of which 2 were waited for; matrix products, arithmetic and copies ran while one was open for 10% of the time, Pallas kernels for 0%

commit v1 on v0

v1 whole, which is shorter than its diff:
```python
import functools

import jax
import jax.numpy as jnp
from jax import lax
from jax.experimental import pallas as pl
from jax.experimental.pallas import tpu as pltpu
from jax.sharding import PartitionSpec as P

NORM_EPS = 1e-6
GELU_K = 0.7978845608028654
GELU_A = 0.044715
F_TILE = 256
ROW_CHUNK = 256
OUT_ROWS = 1024
PLACE_UNROLL = 4
FETCH_TOK = 128
F32 = jnp.float32
BF16 = jnp.bfloat16


def gelu_pair(x):
    sq = x * x
    t = jnp.tanh(x * (GELU_K + (GELU_K * GELU_A) * sq))
    cdf = 0.5 + 0.5 * t
    slope = cdf + (0.5 * x) * (1.0 - t * t) * (GELU_K + (3.0 * GELU_K * GELU_A) * sq)
    return x * cdf, slope


def dot_nn(a, b):
    return lax.dot_general(a, b, (((1,), (0,)), ((), ())), preferred_element_type=F32)


def dot_nt(a, b):
    return lax.dot_general(a, b, (((1,), (1,)), ((), ())), preferred_element_type=F32)


def row_chunks(rows):
    return [pl.ds(r, ROW_CHUNK) for r in range(0, rows, ROW_CHUNK)]


def forward_body(n_layers, n_tiles, x_ref, e_ref, wu_ref, wd_ref, wg_ref, wp_ref, out_ref, xs_ref, dg_ref, gp_ref, x_s, u_s, acc_s):
    layer, tile = pl.program_id(0), pl.program_id(1)
    chunks = row_chunks(x_s.shape[0])

    @pl.when((layer == 0) & (tile == 0))
    def _():
        x_s[...] = x_ref[...]

    @pl.when(tile == 0)
    def _():
        for r in chunks:
            x_bf = x_s[r, :]
            xs_ref[0, r, :] = x_bf
            x_f = x_bf.astype(F32)
            u = (x_f * lax.rsqrt(jnp.mean(x_f * x_f, axis=-1, keepdims=True) + NORM_EPS)).astype(BF16)
            u_s[r, :] = u
            gate_pre = dot_nn(u, wg_ref[0])
            gp_ref[0, r, :] = gate_pre
            gate_act, _ = gelu_pair(gate_pre)
            mixed = (gate_act * e_ref[0, r, :].astype(F32)).astype(BF16)
            acc_s[r, :] = x_f + dot_nn(mixed, wp_ref[0])

    for r in chunks:
        up = dot_nn(u_s[r, :], wu_ref[0])
        act, slope = gelu_pair(up)
        dg_ref[0, 0, r, :] = slope
        acc_s[r, :] += dot_nn(act.astype(BF16), wd_ref[0])

    @pl.when(tile == n_tiles - 1)
    def _():
        x_s[...] = acc_s[...].astype(BF16)

    @pl.when((tile == n_tiles - 1) & (layer == n_layers - 1))
    def _():
        out_ref[...] = x_s[...]


def run_forward(resid_in, fetched, w_up, w_down, w_gate, w_proj):
    n_layers, d_model, ffn = w_up.shape
    rows, e_dim = resid_in.shape[0], w_gate.shape[2]
    n_tiles = ffn // F_TILE
    whole = pl.BlockSpec((rows, d_model), lambda l, j: (0, 0))
    per_layer = lambda *s: pl.BlockSpec((1,) + s, lambda l, j: (l, 0, 0))
    return pl.pallas_call(
        functools.partial(forward_body, n_layers, n_tiles),
        grid=(n_layers, n_tiles),
        in_specs=[
            whole,
            per_layer(rows, e_dim),
            pl.BlockSpec((1, d_model, F_TILE), lambda l, j: (l, 0, j)),
            pl.BlockSpec((1, F_TILE, d_model), lambda l, j: (l, j, 0)),
            per_layer(d_model, e_dim),
            per_layer(e_dim, d_model),
        ],
        out_specs=[
            whole,
            per_layer(rows, d_model),
            pl.BlockSpec((1, 1, rows, F_TILE), lambda l, j: (l, j, 0, 0)),
            per_layer(rows, e_dim),
        ],
        out_shape=[
            jax.ShapeDtypeStruct((rows, d_model), BF16),
            jax.ShapeDtypeStruct((n_layers, rows, d_model), BF16),
            jax.ShapeDtypeStruct((n_layers, n_tiles, rows, F_TILE), F32),
            jax.ShapeDtypeStruct((n_layers, rows, e_dim), F32),
        ],
        scratch_shapes=[pltpu.VMEM((rows, d_model), BF16), pltpu.VMEM((rows, d_model), BF16), pltpu.VMEM((rows, d_model), F32)],
        cost_estimate=pl.CostEstimate(flops=4 * n_layers * rows * d_model * ffn, bytes_accessed=n_layers * 40_000_000, transcendentals=0),
        compiler_params=pltpu.CompilerParams(dimension_semantics=('arbitrary', 'arbitrary'), vmem_limit_bytes=56 * 2**20),
        name='forward',
    )(resid_in, fetched, w_up, w_down, w_gate, w_proj)


def backward_body(n_tiles, c_ref, xs_ref, e_ref, gp_ref, dg_ref, wu_ref, wd_ref, wg_ref, wp_ref, cot_ref, gr_ref, dng_s, acc_s):
    tile = pl.program_id(0)
    chunks = row_chunks(c_ref.shape[0])

    @pl.when(tile == 0)
    def _():
        for r in chunks:
            d_mixed = dot_nt(c_ref[r, :], wp_ref[0]).astype(BF16).astype(F32)
            gate_act, slope = gelu_pair(gp_ref[0, r, :])
            gr_ref[r, :] = gate_act * d_mixed
            d_gate = (slope * (d_mixed * e_ref[0, r, :].astype(F32))).astype(BF16)
            dng_s[r, :] = dot_nt(d_gate, wg_ref[0]).astype(BF16)
            acc_s[r, :] = jnp.zeros((ROW_CHUNK, acc_s.shape[1]), F32)

    for r in chunks:
        d_hidden = dot_nt(c_ref[r, :], wd_ref[0]).astype(BF16).astype(F32)
        d_up = (d_hidden * dg_ref[0, 0, r, :]).astype(BF16)
        acc_s[r, :] += dot_nt(d_up, wu_ref[0])

    @pl.when(tile == n_tiles - 1)
    def _():
        for r in chunks:
            d_n = (acc_s[r, :].astype(BF16).astype(F32) + dng_s[r, :].astype(F32)).astype(BF16).astype(F32)
            x_f = xs_ref[0, r, :].astype(F32)
            inv = lax.rsqrt(jnp.mean(x_f * x_f, axis=-1, keepdims=True) + NORM_EPS)
            proj = jnp.mean(d_n * x_f, axis=-1, keepdims=True)
            d_x = d_n * inv - x_f * (inv * inv * inv * proj)
            cot_ref[r, :] = (c_ref[r, :].astype(F32) + d_x).astype(BF16)


def run_backward(layer, cot, xs, fetched, gp, dg, w_up, w_down, w_gate, w_proj):
    _, d_model, ffn = w_up.shape
    rows, e_dim = cot.shape[0], w_gate.shape[2]
    n_tiles = ffn // F_TILE
    whole = lambda *s: pl.BlockSpec(s, lambda j: (0, 0))
    at_layer = lambda *s: pl.BlockSpec((1,) + s, lambda j: (layer, 0, 0))
    return pl.pallas_call(
        functools.partial(backward_body, n_tiles),
        grid=(n_tiles,),
        in_specs=[
            whole(rows, d_model),
            at_layer(rows, d_model),
            at_layer(rows, e_dim),
            at_layer(rows, e_dim),
            pl.BlockSpec((1, 1, rows, F_TILE), lambda j: (layer, j, 0, 0)),
            pl.BlockSpec((1, d_model, F_TILE), lambda j: (layer, 0, j)),
            pl.BlockSpec((1, F_TILE, d_model), lambda j: (layer, j, 0)),
            at_layer(d_model, e_dim),
            at_layer(e_dim, d_model),
        ],
        out_specs=[whole(rows, d_model), whole(rows, e_dim)],
        out_shape=[jax.ShapeDtypeStruct((rows, d_model), BF16), jax.ShapeDtypeStruct((rows, e_dim), F32)],
        scratch_shapes=[pltpu.VMEM((rows, d_model), BF16), pltpu.VMEM((rows, d_model), F32)],
        cost_estimate=pl.CostEstimate(flops=4 * rows * d_model * ffn, bytes_accessed=40_000_000, transcendentals=0),
        compiler_params=pltpu.CompilerParams(dimension_semantics=('arbitrary',), vmem_limit_bytes=56 * 2**20),
        name='backward',
    )(cot, xs, fetched, gp, dg, w_up, w_down, w_gate, w_proj)


def fetch_body(n_layers, n_tok, n_steps, off_ref, table_ref, out_ref, buf, sems):
    step = pl.program_id(0)

    def issue(at, slot):
        def go(i, carry):
            for k in range(8):
                tok = i * 8 + k
                tile = off_ref[at * n_tok + tok] // 8
                pltpu.make_async_copy(table_ref.at[:, pl.ds(pl.multiple_of(tile * 8, 8), 8), :], buf.at[slot, tok], sems.at[slot]).start()
            return carry

        lax.fori_loop(0, n_tok // 8, go, 0)

    @pl.when(step == 0)
    def _():
        issue(0, 0)

    @pl.when(step + 1 < n_steps)
    def _():
        issue(step + 1, (step + 1) % 2)

    slot = step % 2
    pltpu.make_async_copy(buf.at[slot], buf.at[slot], sems.at[slot]).wait()
    sub = lax.broadcasted_iota(jnp.int32, (8, 128), 0)

    def pick(i, carry):
        halves = [[None, None] for _ in range(n_layers)]
        for half in range(2):
            for k in range(8):
                tok = i * 16 + half * 8 + k
                shift = (k + 8 - off_ref[step * n_tok + tok] % 8) % 8
                for l in range(n_layers):
                    moved = pltpu.roll(buf[slot, tok, l].astype(F32), shift, axis=0)
                    halves[l][half] = moved if k == 0 else jnp.where(sub == k, moved, halves[l][half])
        for l in range(n_layers):
            out_ref[l, pl.ds(pl.multiple_of(i * 16, 16), 16), :] = jnp.concatenate(halves[l], axis=0).astype(BF16)
        return carry

    lax.fori_loop(0, n_tok // 16, pick, 0)


def run_fetch(tables, offsets):
    n_layers, _, e_dim = tables.shape
    n_rows = offsets.shape[0]
    n_steps = n_rows // FETCH_TOK
    return pl.pallas_call(
        functools.partial(fetch_body, n_layers, FETCH_TOK, n_steps),
        grid_spec=pltpu.PrefetchScalarGridSpec(
            num_scalar_prefetch=1,
            grid=(n_steps,),
            in_specs=[pl.BlockSpec(memory_space=pl.ANY)],
            out_specs=pl.BlockSpec((n_layers, FETCH_TOK, e_dim), lambda i, off: (0, i, 0)),
            scratch_shapes=[pltpu.VMEM((2, FETCH_TOK, n_layers, 8, e_dim), BF16), pltpu.SemaphoreType.DMA((2,))],
        ),
        out_shape=jax.ShapeDtypeStruct((n_layers, n_rows, e_dim), BF16),
        cost_estimate=pl.CostEstimate(flops=2_000_000_000, bytes_accessed=30_000_000, transcendentals=0),
        compiler_params=pltpu.CompilerParams(dimension_semantics=('arbitrary',)),
        name='fetch_rows',
    )(offsets, tables)


def place_body(n_group, idx_bits, starts_ref, keys_ref, *refs):
    rows_refs, out_ref = refs[:n_group], refs[-1]
    block = pl.program_id(0)
    out_ref[...] = jnp.zeros_like(out_ref)
    start, end = starts_ref[block], starts_ref[block + 1]
    base = block * OUT_ROWS

    def go(i, carry):
        prev, accs = carry[0], list(carry[1:])
        for u in range(PLACE_UNROLL):
            k = start + i * PLACE_UNROLL + u
            key = keys_ref[jnp.minimum(k, end - 1)]
            src = key & ((1 << idx_bits) - 1)
            row_id = key >> idx_bits
            fresh, live = row_id != prev, k < end
            for g in range(n_group):
                row = jnp.where(live, rows_refs[g][pl.ds(src, 1), :], 0.0)
                accs[g] = row + jnp.where(fresh, 0.0, accs[g])
                out_ref[g, pl.ds(row_id - base, 1), :] = accs[g]
            prev = row_id
        return (prev, *accs)

    zero = jnp.zeros((1, out_ref.shape[2]), F32)
    lax.fori_loop(0, (end - start + PLACE_UNROLL - 1) // PLACE_UNROLL, go, (jnp.int32(-1),) + (zero,) * n_group)


def run_place(group, starts, keys, rows_list, d_tables, shape):
    n_group = len(rows_list)
    n_rows, e_dim = rows_list[0].shape
    idx_bits = (n_rows - 1).bit_length()
    args = [starts, keys, *rows_list]
    in_specs = [pl.BlockSpec((n_rows, e_dim), lambda i, s, k: (0, 0)) for _ in rows_list]
    aliases = {}
    if d_tables is not None:
        aliases = {len(args): 0}
        args.append(d_tables)
        in_specs.append(pl.BlockSpec(memory_space=pl.ANY))
    return pl.pallas_call(
        functools.partial(place_body, n_group, idx_bits),
        grid_spec=pltpu.PrefetchScalarGridSpec(
            num_scalar_prefetch=2,
            grid=(pl.cdiv(shape[1], OUT_ROWS),),
            in_specs=in_specs,
            out_specs=pl.BlockSpec((n_group, OUT_ROWS, e_dim), lambda i, s, k: (group, i, 0)),
        ),
        out_shape=jax.ShapeDtypeStruct(shape, F32),
        input_output_aliases=aliases,
        cost_estimate=pl.CostEstimate(flops=30_000_000_000, bytes_accessed=n_group * 44_000_000, transcendentals=0),
        compiler_params=pltpu.CompilerParams(dimension_semantics=('arbitrary',), vmem_limit_bytes=48 * 2**20),
        name='place_rows',
    )(*args)


def solution(mesh):
    n_emb = mesh.shape['emb']
    tok_spec = P(('dp', 'emb'))
    act_spec = P(('dp', 'emb'), None)
    table_spec = P(None, 'emb', None)
    full_spec = P(None, None, None)
    swap = [(i, (i + 1) % n_emb) for i in range(n_emb)]

    def device_body(tok_ids, resid_in, cot_out, tables, w_up, w_down, w_gate, w_proj):
        n_layers, range_rows, e_dim = tables.shape
        tok_count = tok_ids.shape[0]
        base = lax.axis_index('emb') * range_rows

        own_off = tok_ids - base
        own_mask = (own_off >= 0) & (own_off < range_rows)
        peer_ids = lax.ppermute(tok_ids, 'emb', swap)
        offsets = jnp.clip(jnp.concatenate([own_off, peer_ids - base]), 0, range_rows - 1)
        served = run_fetch(tables, offsets)
        from_peer = lax.ppermute(served[:, tok_count:], 'emb', swap)
        fetched = jnp.where(own_mask[None, :, None], served[:, :tok_count], from_peer)

        all_ids = lax.all_gather(tok_ids, ('dp', 'emb'), axis=0, tiled=True)
        n_all = all_ids.shape[0]
        idx_bits = (n_all - 1).bit_length()
        all_off = all_ids - base
        all_off = jnp.where((all_off >= 0) & (all_off < range_rows), all_off, range_rows)
        keys = jnp.sort((all_off << idx_bits) | jnp.arange(n_all, dtype=jnp.int32))
        n_blocks = pl.cdiv(range_rows, OUT_ROWS)
        bounds = jnp.minimum(jnp.arange(n_blocks + 1, dtype=jnp.int32) * OUT_ROWS, range_rows)
        starts = jnp.sum((all_off[None, :] < bounds[:, None]).astype(jnp.int32), axis=1)

        resid_out, xs, dg, gp = run_forward(resid_in, fetched, w_up, w_down, w_gate, w_proj)

        cot = cot_out
        rows_list = [None] * n_layers
        for layer in reversed(range(n_layers)):
            cot, grad_rows = run_backward(layer, cot, xs, fetched, gp, dg, w_up, w_down, w_gate, w_proj)
            rows_list[layer] = lax.all_gather(grad_rows, ('dp', 'emb'), axis=0, tiled=True)

        d_tables = None
        per_group = n_layers // 2
        for group in (1, 0):
            d_tables = run_place(group, starts, keys, rows_list[group * per_group:(group + 1) * per_group], d_tables, tables.shape)
        return resid_out, d_tables

    return jax.shard_map(device_body, mesh=mesh, in_specs=(tok_spec, act_spec, act_spec, table_spec, full_spec, full_spec, full_spec, full_spec), out_specs=(act_spec, table_spec), check_vma=False)
```

time: 4700 us -> 767 us (0.16)
  waiting for transfers between devices: 3630 us -> 3.83 us
  Pallas kernels: 0 us -> 675 us
  matrix products: 470 us -> 0 us
  local copies, waits for them, and re-layouts: 362 us -> 6.05 us
  other arithmetic: 161 us -> 10 us
    psum x2 -> x0, waiting for transfers between devices: 3630 us -> none  [device_body(): grad_list[l_idx] = lax.psum(shard_grad, 'dp')]
    pallas_call x0 -> x10, Pallas kernels: none -> 675 us  [the longest x6 239 us: run_backward(): pl.pallas_call(functools.partial(backward_body, n_tiles), grid=(n_tiles,)...]
    dot_general x45 -> x0, matrix products: 470 us -> none  [the longest x6 131 us: layer_forward(): mlp_out = jnp.dot(hidden, w_down_l, preferred_element_type=jnp.float32)]
    scatter-add x6 -> x0, other arithmetic: 147 us -> none  [device_body(): jax.ops.segment_sum(incoming, recv_ids, num_segments=range_rows)]
    unnamed x178 -> x8, local copies, waits for them, and re-layouts: 147 us -> 4.38 us
    gather x19 -> x0, local copies, waits for them, and re-layouts: 119 us -> none  [the longest x6 70.2 us: device_body(): served = jnp.take(tables[l_idx], recv_ids, axis=0)]
    squeeze x1 -> x0, local copies, waits for them, and re-layouts: 75.3 us -> none  [device_body(): served = jnp.take(tables[l_idx], recv_ids, axis=0)]
  transfers between devices with their start and end apart: 12 -> 8, of which waited for: 2 -> 2; matrix products, arithmetic and copies ran while one was open for 10% -> 1% of each run, Pallas kernels for 0% -> 37%
where the time goes in v1:
time: 767 us; the launch traced here: 758 us
  Pallas kernels  675 us (88%)
  starting transfers between devices  33.5 us (4%)
  blocking collectives  14.6 us (2%)
  between operations  14.6 us (2%)
  other arithmetic  10 us (1%)
    pallas_call x6, Pallas kernels, run_backward(): pl.pallas_call(functools.partial(backward_body, n_tiles), grid=(n_tiles,)...  239 us
    pallas_call x1, Pallas kernels, run_forward(): pl.pallas_call(functools.partial(forward_body, n_layers, n_tiles), grid=(...  225 us
    pallas_call x2, Pallas kernels, run_place(): pl.pallas_call(functools.partial(place_body, n_group, idx_bits), grid_spe...  167 us
    pallas_call x1, Pallas kernels, run_fetch(): pl.pallas_call(functools.partial(fetch_body, n_layers, FETCH_TOK, n_steps...  43.4 us
    ppermute x1, starting transfers between devices, device_body(): from_peer = lax.ppermute(served[:, tok_count:], 'emb', swap)  21.2 us
  transfers between devices with their start and end apart: 8, of which 2 were waited for; matrix products, arithmetic and copies ran while one was open for 1% of the time, Pallas kernels for 37%

profile of v1, /device:TPU:0, one launch (start us, length us, event | category | flops | bytes accessed | tf_op | source)
XLA Modules:
  0.0 757.8 jit_solution(11729667623015765099)
XLA Ops:
  7.2 0.0 all-gather.17.cloned.1.call-start
  7.2 0.9 collective-permute-start
  8.1 0.7 compare_and_fusion
  8.8 0.1 collective-permute-done
  8.9 0.6 add_clamp_fusion.off_ref
  9.5 43.4 %fetch_rows.1 = bf16[6,2048,128]{2,1,0:T(8,128)(2,1)} custom-call(s32[2048]{0:T(1024)} %add_clamp_fusion.off_ref, bf16[6,75968,128]{2,1,0:T(8,128)(2,1)} %table_ref.1), custom_call_target="tpu_custom_call" | custom-call | flops 2000000000 | bytes 30000000 | tf_op jit(solution)/shard_map/fetch_rows/pallas_call | solution.py:219
  52.9 0.0 copy-start.2
  52.9 1.7 slice.9
  54.6 21.2 %collective-permute-start.1 = (bf16[6,1024,128]{2,1,0:T(8,128)(2,1)S(1)}, bf16[6,1024,128]{2,1,0:T(8,128)(2,1)S(1)}, u32[]{:S(2)}, u32[]{:S(2)}) collective-permute-start(bf16[6,1024,128]{2,1,0:T(8,128)(2,1)S(1)} %slice.9), channel_id=1, source_target_pairs={{0,1},{1,0},{2,3},{3,2},{4,5},{5,4},{6,7},{7,6}} | collective-permute-start | bytes 4718600 | tf_op jit(solution)/shard_map/ppermute | solution.py:306
  75.8 3.0 collective-permute-done.1
  78.8 0.0 copy-done.2
  78.8 1.4 slice_select_fusion.e_ref
  80.2 225.2 %forward.1 = (bf16[1024,896]{1,0:T(8,128)(2,1)}, bf16[6,1024,896]{2,1,0:T(8,128)(2,1)}, f32[6,19,1024,256]{3,2,1,0:T(8,128)}, f32[6,1024,128]{2,1,0:T(8,128)}) custom-call(bf16[1024,896]{1,0:T(8,128)(2,1)} %x_ref.1, bf16[6,1024,128]{2,1,0:T(8,128)(2,1)} %slice_select_fusion.e_ref, bf16[6,896,4864]{2,1,0:T(8,128)(2,1)} %wu_ref.13, ...), custom_call_target="tpu_custom_call" | custom-call | flops 107105746944 | bytes 240000000 | tf_op jit(solution)/shard_map/forward/pallas_call | solution.py:85
  305.4 39.8 %backward.6 = (bf16[1024,896]{1,0:T(8,128)(2,1)}, f32[1024,128]{1,0:T(8,128)}) custom-call(bf16[1024,896]{1,0:T(8,128)(2,1)} %c_ref.1, bf16[6,1024,896]{2,1,0:T(8,128)(2,1)} %get-tuple-element.21.xs_ref, bf16[6,1024,128]{2,1,0:T(8,128)(2,1)} %slice_select_fusion.e_ref, f32[6,1024,128]{2,1,0:T(8,128)} %get-tuple-element.22.gp_ref, ...), custom_call_target="tpu_custom_call" | custom-call | flops 17850957824 | bytes 40000000 | tf_op jit(solution)/shard_map/backward/pallas_call | solution.py:151
  345.2 0.0 all-gather.17.cloned.1.call-update
  345.3 11.0 %all-gather.15.cloned.1.call-start = ((), (), s32[]{:S(2)}) async-start(), calls=%async_computation.4 | async-start | bytes 4718592 | tf_op jit(solution)/shard_map/all_gather | solution.py:325
  356.3 39.9 %backward.7 = (bf16[1024,896]{1,0:T(8,128)(2,1)}, f32[1024,128]{1,0:T(8,128)}) custom-call(bf16[1024,896]{1,0:T(8,128)(2,1)} %get-tuple-element.24.c_ref, bf16[6,1024,896]{2,1,0:T(8,128)(2,1)} %get-tuple-element.21.xs_ref, bf16[6,1024,128]{2,1,0:T(8,128)(2,1)} %slice_select_fusion.e_ref, f32[6,1024,128]{2,1,0:T(8,128)} %get-tuple-element.22.gp_ref, ...), custom_call_target="tpu_custom_call" | custom-call | flops 17850957824 | bytes 40000000 | tf_op jit(solution)/shard_map/backward/pallas_call | solution.py:151
  396.2 0.0 all-gather.15.cloned.1.call-update
  396.2 0.0 all-gather.13.cloned.1.call-start
  396.3 39.9 %backward.8 = (bf16[1024,896]{1,0:T(8,128)(2,1)}, f32[1024,128]{1,0:T(8,128)}) custom-call(bf16[1024,896]{1,0:T(8,128)(2,1)} %get-tuple-element.25.c_ref, bf16[6,1024,896]{2,1,0:T(8,128)(2,1)} %get-tuple-element.21.xs_ref, bf16[6,1024,128]{2,1,0:T(8,128)(2,1)} %slice_select_fusion.e_ref, f32[6,1024,128]{2,1,0:T(8,128)} %get-tuple-element.22.gp_ref, ...), custom_call_target="tpu_custom_call" | custom-call | flops 17850957824 | bytes 40000000 | tf_op jit(solution)/shard_map/backward/pallas_call | solution.py:151
  436.2 0.0 all-gather.13.cloned.1.call-update
  436.2 0.0 all-gather.11.cloned.1.call-start
  436.2 39.8 %backward.9 = (bf16[1024,896]{1,0:T(8,128)(2,1)}, f32[1024,128]{1,0:T(8,128)}) custom-call(bf16[1024,896]{1,0:T(8,128)(2,1)} %get-tuple-element.26.c_ref, bf16[6,1024,896]{2,1,0:T(8,128)(2,1)} %get-tuple-element.21.xs_ref, bf16[6,1024,128]{2,1,0:T(8,128)(2,1)} %slice_select_fusion.e_ref, f32[6,1024,128]{2,1,0:T(8,128)} %get-tuple-element.22.gp_ref, ...), custom_call_target="tpu_custom_call" | custom-call | flops 17850957824 | bytes 40000000 | tf_op jit(solution)/shard_map/backward/pallas_call | solution.py:151
  476.1 0.0 all-gather.11.cloned.1.call-update
  476.1 0.2 all-gather.7.cloned.1.call-start
  476.3 39.8 %backward.10 = (bf16[1024,896]{1,0:T(8,128)(2,1)}, f32[1024,128]{1,0:T(8,128)}) custom-call(bf16[1024,896]{1,0:T(8,128)(2,1)} %get-tuple-element.27.c_ref, bf16[6,1024,896]{2,1,0:T(8,128)(2,1)} %get-tuple-element.21.xs_ref, bf16[6,1024,128]{2,1,0:T(8,128)(2,1)} %slice_select_fusion.e_ref, f32[6,1024,128]{2,1,0:T(8,128)} %get-tuple-element.22.gp_ref, ...), custom_call_target="tpu_custom_call" | custom-call | flops 17850957824 | bytes 40000000 | tf_op jit(solution)/shard_map/backward/pallas_call | solution.py:151
  516.2 0.0 copy-start.3
  516.2 39.9 %backward.11 = (bf16[1024,896]{1,0:T(8,128)(2,1)}, f32[1024,128]{1,0:T(8,128)}) custom-call(bf16[1024,896]{1,0:T(8,128)(2,1)} %get-tuple-element.28.c_ref, bf16[6,1024,896]{2,1,0:T(8,128)(2,1)} %get-tuple-element.21.xs_ref, bf16[6,1024,128]{2,1,0:T(8,128)(2,1)} %slice_select_fusion.e_ref, f32[6,1024,128]{2,1,0:T(8,128)} %get-tuple-element.22.gp_ref, ...), custom_call_target="tpu_custom_call" | custom-call | flops 17850957824 | bytes 40000000 | tf_op jit(solution)/shard_map/backward/pallas_call | solution.py:151
  556.0 0.0 all-gather.7.cloned.1.call-update
  556.1 0.0 all-gather.9.cloned.1.call-start
  556.1 0.5 all-gather.9.cloned.1.call-update
  556.6 0.0 copy-done.3
  556.7 14.6 %all_gather.21 = s32[8192]{0:T(1024)S(1)} all-gather(s32[1024]{0:T(1024)S(1)} %copy-done.3), channel_id=1, replica_groups=mesh['dp'=4,'emb'=2] {'dp','emb'}, dimensions={0}, use_global_device_ids=true | all-gather | bytes 36864 | tf_op jit(solution)/shard_map/all_gather | solution.py:309
  571.3 6.8 sort.14
  578.1 0.5 convert_reduce_fusion.starts_ref
  578.6 0.0 all-gather.17.cloned.1.call-done.refs_2_
  578.7 0.0 all-gather.15.cloned.1.call-done.refs_1_
  578.7 0.0 all-gather.13.cloned.1.call-done.refs_0_
  578.7 0.0 copy-start
  578.7 2.2 copy-done
  580.9 83.7 %place_rows.2.refs_3_ = f32[6,75968,128]{2,1,0:T(8,128)} custom-call(s32[76]{0:T(128)S(1)} %convert_reduce_fusion.starts_ref, s32[8192]{0:T(1024)S(1)} %get-tuple-element.20.keys_ref, f32[8192,128]{1,0:T(8,128)S(1)} %copy-done, f32[8192,128]{1,0:T(8,128)} %all-gather.15.cloned.1.call-done.refs_1_, f32[8192,128]{1,0:T(8,128)} %all-gather.17.cloned.1.call-done.refs_2_), custom_call_target="tpu_custom_call" | custom-call | flops 30000001024 | bytes 132000000 | tf_op jit(solution)/shard_map/place_rows/pallas_call | solution.py:272
  664.6 0.0 all-gather.11.cloned.1.call-done.refs_2_
  664.6 0.0 all-gather.7.cloned.1.call-done.refs_0_
  664.6 0.0 all-gather.9.cloned.1.call-done.refs_1_
  664.6 0.0 copy-start.1
  664.6 2.2 copy-done.1
  666.8 83.7 %place_rows.3 = f32[6,75968,128]{2,1,0:T(8,128)} custom-call(s32[76]{0:T(128)S(1)} %convert_reduce_fusion.starts_ref, s32[8192]{0:T(1024)S(1)} %get-tuple-element.20.keys_ref, f32[8192,128]{1,0:T(8,128)S(1)} %copy-done.1, f32[8192,128]{1,0:T(8,128)} %all-gather.9.cloned.1.call-done.refs_1_, ...), custom_call_target="tpu_custom_call", output_to_operand_aliasing={{}: (5, {})} | custom-call | flops 30000001024 | bytes 132000000 | tf_op jit(solution)/shard_map/place_rows/pallas_call | solution.py:272
  (4 shorter events, 0.0 us)
Async XLA Ops:
  7.2 571.5 %all-gather.17.cloned.1.call-start = ((), (), s32[]{:S(2)}) async-start(), calls=%async_computation.5 | async-start | bytes 4718592 | tf_op jit(solution)/shard_map/all_gather | solution.py:325
  7.2 1.7 collective-permute-start
  52.9 26.0 %copy-start.2 = (bf16[6,2048,128]{2,1,0:T(8,128)(2,1)S(1)}, bf16[6,2048,128]{2,1,0:T(8,128)(2,1)}, u32[]{:S(2)}) copy-start(bf16[6,2048,128]{2,1,0:T(8,128)(2,1)} %fetch_rows.1) | copy-start | bytes 9437188
  54.6 24.3 %collective-permute-start.1 = (bf16[6,1024,128]{2,1,0:T(8,128)(2,1)S(1)}, bf16[6,1024,128]{2,1,0:T(8,128)(2,1)S(1)}, u32[]{:S(2)}, u32[]{:S(2)}) collective-permute-start(bf16[6,1024,128]{2,1,0:T(8,128)(2,1)S(1)} %slice.9), channel_id=1, source_target_pairs={{0,1},{1,0},{2,3},{3,2},{4,5},{5,4},{6,7},{7,6}} | collective-permute-start | bytes 4718600 | tf_op jit(solution)/shard_map/ppermute | solution.py:306
  345.3 233.4 %all-gather.15.cloned.1.call-start = ((), (), s32[]{:S(2)}) async-start(), calls=%async_computation.4 | async-start | bytes 4718592 | tf_op jit(solution)/shard_map/all_gather | solution.py:325
  396.2 182.5 %all-gather.13.cloned.1.call-start = ((), (), s32[]{:S(2)}) async-start(), calls=%async_computation.3 | async-start | bytes 4718592 | tf_op jit(solution)/shard_map/all_gather | solution.py:325
  436.2 228.4 %all-gather.11.cloned.1.call-start = ((), (), s32[]{:S(2)}) async-start(), calls=%async_computation.2 | async-start | bytes 4718592 | tf_op jit(solution)/shard_map/all_gather | solution.py:325
  476.1 188.5 %all-gather.7.cloned.1.call-start = ((), (), s32[]{:S(2)}) async-start(), calls=%async_computation | async-start | bytes 4718592 | tf_op jit(solution)/shard_map/all_gather | solution.py:325
  516.2 40.5 %copy-start.3 = (s32[1024]{0:T(1024)S(1)}, s32[1024]{0:T(1024)}, u32[]{:S(2)}) copy-start(s32[1024]{0:T(1024)} %param.8) | copy-start | bytes 12292
  556.1 108.5 %all-gather.9.cloned.1.call-start = ((), (), s32[]{:S(2)}) async-start(), calls=%async_computation.1 | async-start | bytes 4718592 | tf_op jit(solution)/shard_map/all_gather | solution.py:325
  578.7 2.2 copy-start
  664.6 2.2 copy-start.1
Sparse Core Ops, SparseCore 0:
  345.4 33.7 all-gather.16
  396.3 33.7 all-gather.14
  436.3 33.7 all-gather.12
  476.2 33.7 all-gather.10
  556.2 34.7 all-gather.6
  592.7 30.7 all-gather.8

commit v2 on v1

--- a/solution.py
+++ b/solution.py
@@ -11,9 +11,11 @@
 GELU_K = 0.7978845608028654
 GELU_A = 0.044715
 F_TILE = 256
-ROW_CHUNK = 256
+FWD_CHUNK = 256
+BWD_CHUNK = 1024
 OUT_ROWS = 1024
-PLACE_UNROLL = 4
+PLACE_UNROLL = 8
+PLACE_BUFS = 4
 FETCH_TOK = 128
 F32 = jnp.float32
 BF16 = jnp.bfloat16
@@ -35,13 +37,21 @@
     return lax.dot_general(a, b, (((1,), (1,)), ((), ())), preferred_element_type=F32)
 
 
-def row_chunks(rows):
-    return [pl.ds(r, ROW_CHUNK) for r in range(0, rows, ROW_CHUNK)]
-
-
-def forward_body(n_layers, n_tiles, x_ref, e_ref, wu_ref, wd_ref, wg_ref, wp_ref, out_ref, xs_ref, dg_ref, gp_ref, x_s, u_s, acc_s):
+def row_chunks(rows, size):
+    return [pl.ds(r, min(size, rows)) for r in range(0, rows, size)]
+
+
+def forward_body(n_layers, n_tiles, x_ref, e_ref, wu_ref, wd_ref, wg_ref, wp_ref, out_ref, xs_ref, dg_ref, gp_ref, x_s, u_s, h_s, acc_s):
     layer, tile = pl.program_id(0), pl.program_id(1)
-    chunks = row_chunks(x_s.shape[0])
+    chunks = row_chunks(x_s.shape[0], FWD_CHUNK)
+
+    def up_half(r):
+        act, slope = gelu_pair(dot_nn(u_s[r, :], wu_ref[0]))
+        dg_ref[0, 0, r, :] = slope
+        h_s[r, :] = act.astype(BF16)
+
+    def down_half(r):
+        acc_s[r, :] += dot_nn(h_s[r, :], wd_ref[0])
 
     @pl.when((layer == 0) & (tile == 0))
     def _():
@@ -60,18 +70,20 @@
             gate_act, _ = gelu_pair(gate_pre)
             mixed = (gate_act * e_ref[0, r, :].astype(F32)).astype(BF16)
             acc_s[r, :] = x_f + dot_nn(mixed, wp_ref[0])
-
-    for r in chunks:
-        up = dot_nn(u_s[r, :], wu_ref[0])
-        act, slope = gelu_pair(up)
-        dg_ref[0, 0, r, :] = slope
-        acc_s[r, :] += dot_nn(act.astype(BF16), wd_ref[0])
-
-    @pl.when(tile == n_tiles - 1)
-    def _():
-        x_s[...] = acc_s[...].astype(BF16)
-
-    @pl.when((tile == n_tiles - 1) & (layer == n_layers - 1))
+            up_half(r)
+
+    @pl.when((tile > 0) & (tile < n_tiles))
+    def _():
+        for r in chunks:
+            down_half(r)
+            up_half(r)
+
+    @pl.when(tile == n_tiles)
+    def _():
+        for r in chunks:
+            x_s[r, :] = (acc_s[r, :] + dot_nn(h_s[r, :], wd_ref[0])).astype(BF16)
+
+    @pl.when((tile == n_tiles) & (layer == n_layers - 1))
     def _():
         out_ref[...] = x_s[...]
 
@@ -84,19 +96,19 @@
     per_layer = lambda *s: pl.BlockSpec((1,) + s, lambda l, j: (l, 0, 0))
     return pl.pallas_call(
         functools.partial(forward_body, n_layers, n_tiles),
-        grid=(n_layers, n_tiles),
+        grid=(n_layers, n_tiles + 1),
         in_specs=[
             whole,
             per_layer(rows, e_dim),
-            pl.BlockSpec((1, d_model, F_TILE), lambda l, j: (l, 0, j)),
-            pl.BlockSpec((1, F_TILE, d_model), lambda l, j: (l, j, 0)),
+            pl.BlockSpec((1, d_model, F_TILE), lambda l, j: (l, 0, jnp.minimum(j, n_tiles - 1))),
+            pl.BlockSpec((1, F_TILE, d_model), lambda l, j: (l, jnp.maximum(j - 1, 0), 0)),
             per_layer(d_model, e_dim),
             per_layer(e_dim, d_model),
         ],
         out_specs=[
             whole,
             per_layer(rows, d_model),
-            pl.BlockSpec((1, 1, rows, F_TILE), lambda l, j: (l, j, 0, 0)),
+            pl.BlockSpec((1, 1, rows, F_TILE), lambda l, j: (l, jnp.minimum(j, n_tiles - 1), 0, 0)),
             per_layer(rows, e_dim),
         ],
         out_shape=[
@@ -105,16 +117,20 @@
             jax.ShapeDtypeStruct((n_layers, n_tiles, rows, F_TILE), F32),
             jax.ShapeDtypeStruct((n_layers, rows, e_dim), F32),
         ],
-        scratch_shapes=[pltpu.VMEM((rows, d_model), BF16), pltpu.VMEM((rows, d_model), BF16), pltpu.VMEM((rows, d_model), F32)],
+        scratch_shapes=[pltpu.VMEM((rows, d_model), BF16), pltpu.VMEM((rows, d_model), BF16), pltpu.VMEM((rows, F_TILE), BF16), pltpu.VMEM((rows, d_model), F32)],
         cost_estimate=pl.CostEstimate(flops=4 * n_layers * rows * d_model * ffn, bytes_accessed=n_layers * 40_000_000, transcendentals=0),
         compiler_params=pltpu.CompilerParams(dimension_semantics=('arbitrary', 'arbitrary'), vmem_limit_bytes=56 * 2**20),
         name='forward',
     )(resid_in, fetched, w_up, w_down, w_gate, w_proj)
 
 
-def backward_body(n_tiles, c_ref, xs_ref, e_ref, gp_ref, dg_ref, wu_ref, wd_ref, wg_ref, wp_ref, cot_ref, gr_ref, dng_s, acc_s):
+def backward_body(n_tiles, c_ref, xs_ref, e_ref, gp_ref, dg_ref, wu_ref, wd_ref, wg_ref, wp_ref, cot_ref, gr_ref, dng_s, du_s, acc_s):
     tile = pl.program_id(0)
-    chunks = row_chunks(c_ref.shape[0])
+    chunks = row_chunks(c_ref.shape[0], BWD_CHUNK)
+
+    def hidden_half(r):
+        d_hidden = dot_nt(c_ref[r, :], wd_ref[0]).astype(BF16).astype(F32)
+        du_s[r, :] = (d_hidden * dg_ref[0, 0, r, :]).astype(BF16)
 
     @pl.when(tile == 0)
     def _():
@@ -124,17 +140,20 @@
             gr_ref[r, :] = gate_act * d_mixed
             d_gate = (slope * (d_mixed * e_ref[0, r, :].astype(F32))).astype(BF16)
             dng_s[r, :] = dot_nt(d_gate, wg_ref[0]).astype(BF16)
-            acc_s[r, :] = jnp.zeros((ROW_CHUNK, acc_s.shape[1]), F32)
-
-    for r in chunks:
-        d_hidden = dot_nt(c_ref[r, :], wd_ref[0]).astype(BF16).astype(F32)
-        d_up = (d_hidden * dg_ref[0, 0, r, :]).astype(BF16)
-        acc_s[r, :] += dot_nt(d_up, wu_ref[0])
-
-    @pl.when(tile == n_tiles - 1)
-    def _():
-        for r in chunks:
-            d_n = (acc_s[r, :].astype(BF16).astype(F32) + dng_s[r, :].astype(F32)).astype(BF16).astype(F32)
+            acc_s[r, :] = jnp.zeros((r.size, acc_s.shape[1]), F32)
+            hidden_half(r)
+
+    @pl.when((tile > 0) & (tile < n_tiles))
+    def _():
+        for r in chunks:
+            acc_s[r, :] += dot_nt(du_s[r, :], wu_ref[0])
+            hidden_half(r)
+
+    @pl.when(tile == n_tiles)
+    def _():
+        for r in chunks:
+            acc = acc_s[r, :] + dot_nt(du_s[r, :], wu_ref[0])
+            d_n = (acc.astype(BF16).astype(F32) + dng_s[r, :].astype(F32)).astype(BF16).astype(F32)
             x_f = xs_ref[0, r, :].astype(F32)
             inv = lax.rsqrt(jnp.mean(x_f * x_f, axis=-1, keepdims=True) + NORM_EPS)
             proj = jnp.mean(d_n * x_f, axis=-1, keepdims=True)
@@ -150,21 +169,21 @@
     at_layer = lambda *s: pl.BlockSpec((1,) + s, lambda j: (layer, 0, 0))
     return pl.pallas_call(
         functools.partial(backward_body, n_tiles),
-        grid=(n_tiles,),
+        grid=(n_tiles + 1,),
         in_specs=[
             whole(rows, d_model),
             at_layer(rows, d_model),
             at_layer(rows, e_dim),
             at_layer(rows, e_dim),
-            pl.BlockSpec((1, 1, rows, F_TILE), lambda j: (layer, j, 0, 0)),
-            pl.BlockSpec((1, d_model, F_TILE), lambda j: (layer, 0, j)),
-            pl.BlockSpec((1, F_TILE, d_model), lambda j: (layer, j, 0)),
+            pl.BlockSpec((1, 1, rows, F_TILE), lambda j: (layer, jnp.minimum(j, n_tiles - 1), 0, 0)),
+            pl.BlockSpec((1, d_model, F_TILE), lambda j: (layer, 0, jnp.maximum(j - 1, 0))),
+            pl.BlockSpec((1, F_TILE, d_model), lambda j: (layer, jnp.minimum(j, n_tiles - 1), 0)),
             at_layer(d_model, e_dim),
             at_layer(e_dim, d_model),
         ],
         out_specs=[whole(rows, d_model), whole(rows, e_dim)],
         out_shape=[jax.ShapeDtypeStruct((rows, d_model), BF16), jax.ShapeDtypeStruct((rows, e_dim), F32)],
-        scratch_shapes=[pltpu.VMEM((rows, d_model), BF16), pltpu.VMEM((rows, d_model), F32)],
+        scratch_shapes=[pltpu.VMEM((rows, d_model), BF16), pltpu.VMEM((rows, F_TILE), BF16), pltpu.VMEM((rows, d_model), F32)],
         cost_estimate=pl.CostEstimate(flops=4 * rows * d_model * ffn, bytes_accessed=40_000_000, transcendentals=0),
         compiler_params=pltpu.CompilerParams(dimension_semantics=('arbitrary',), vmem_limit_bytes=56 * 2**20),
         name='backward',
@@ -179,7 +198,7 @@
             for k in range(8):
                 tok = i * 8 + k
                 tile = off_ref[at * n_tok + tok] // 8
-                pltpu.make_async_copy(table_ref.at[:, pl.ds(pl.multiple_of(tile * 8, 8), 8), :], buf.at[slot, tok], sems.at[slot]).start()
+                pltpu.make_async_copy(table_ref.at[:, pl.ds(pl.multiple_of(tile * 8, 8), 8), :], buf.at[slot, tok], sems.at[slot]).start(priority=k % 2)
             return carry
 
         lax.fori_loop(0, n_tok // 8, go, 0)
@@ -232,36 +251,57 @@
     )(offsets, tables)
 
 
-def place_body(n_group, idx_bits, starts_ref, keys_ref, *refs):
-    rows_refs, out_ref = refs[:n_group], refs[-1]
+def place_body(group, n_group, idx_bits, n_blocks, tail, starts_ref, keys_ref, *refs):
+    rows_refs, out_ref, buf, sems = refs[:n_group], refs[-3], refs[-2], refs[-1]
     block = pl.program_id(0)
-    out_ref[...] = jnp.zeros_like(out_ref)
+    slot = block % PLACE_BUFS
+
+    def copy(at, which, rows):
+        where = pl.ds(pl.multiple_of(at * OUT_ROWS, OUT_ROWS), rows)
+        return pltpu.make_async_copy(buf.at[which, :, pl.ds(0, rows), :], out_ref.at[pl.ds(group * n_group, n_group), where, :], sems.at[which])
+
+    @pl.when(block >= PLACE_BUFS)
+    def _():
+        copy(block - PLACE_BUFS, slot, OUT_ROWS).wait()
+
+    buf[slot] = jnp.zeros(buf.shape[1:], F32)
     start, end = starts_ref[block], starts_ref[block + 1]
     base = block * OUT_ROWS
 
     def go(i, carry):
         prev, accs = carry[0], list(carry[1:])
         for u in range(PLACE_UNROLL):
-            k = start + i * PLACE_UNROLL + u
-            key = keys_ref[jnp.minimum(k, end - 1)]
+            key = keys_ref[start + i * PLACE_UNROLL + u]
             src = key & ((1 << idx_bits) - 1)
             row_id = key >> idx_bits
-            fresh, live = row_id != prev, k < end
+            fresh = row_id != prev
+            dst = jnp.minimum(row_id - base, OUT_ROWS)
             for g in range(n_group):
-                row = jnp.where(live, rows_refs[g][pl.ds(src, 1), :], 0.0)
-                accs[g] = row + jnp.where(fresh, 0.0, accs[g])
-                out_ref[g, pl.ds(row_id - base, 1), :] = accs[g]
+                accs[g] = rows_refs[g][pl.ds(src, 1), :] + jnp.where(fresh, 0.0, accs[g])
+                buf[slot, g, pl.ds(dst, 1), :] = accs[g]
             prev = row_id
         return (prev, *accs)
 
-    zero = jnp.zeros((1, out_ref.shape[2]), F32)
+    zero = jnp.zeros((1, buf.shape[3]), F32)
     lax.fori_loop(0, (end - start + PLACE_UNROLL - 1) // PLACE_UNROLL, go, (jnp.int32(-1),) + (zero,) * n_group)
+
+    @pl.when(block < n_blocks - 1)
+    def _():
+        copy(block, slot, OUT_ROWS).start()
+
+    @pl.when(block == n_blocks - 1)
+    def _():
+        copy(block, slot, tail).start()
+        for at in range(max(0, n_blocks - PLACE_BUFS), n_blocks):
+            copy(at, at % PLACE_BUFS, tail if at == n_blocks - 1 else OUT_ROWS).wait()
 
 
 def run_place(group, starts, keys, rows_list, d_tables, shape):
     n_group = len(rows_list)
     n_rows, e_dim = rows_list[0].shape
     idx_bits = (n_rows - 1).bit_length()
+    n_blocks = pl.cdiv(shape[1], OUT_ROWS)
+    tail = shape[1] - (n_blocks - 1) * OUT_ROWS
     args = [starts, keys, *rows_list]
     in_specs = [pl.BlockSpec((n_rows, e_dim), lambda i, s, k: (0, 0)) for _ in rows_list]
     aliases = {}
@@ -270,17 +310,18 @@
         args.append(d_tables)
         in_specs.append(pl.BlockSpec(memory_space=pl.ANY))
     return pl.pallas_call(
-        functools.partial(place_body, n_group, idx_bits),
+        functools.partial(place_body, group, n_group, idx_bits, n_blocks, tail),
         grid_spec=pltpu.PrefetchScalarGridSpec(
             num_scalar_prefetch=2,
-            grid=(pl.cdiv(shape[1], OUT_ROWS),),
+            grid=(n_blocks,),
             in_specs=in_specs,
-            out_specs=pl.BlockSpec((n_group, OUT_ROWS, e_dim), lambda i, s, k: (group, i, 0)),
+            out_specs=pl.BlockSpec(memory_space=pl.ANY),
+            scratch_shapes=[pltpu.VMEM((PLACE_BUFS, n_group, OUT_ROWS + 8, e_dim), F32), pltpu.SemaphoreType.DMA((PLACE_BUFS,))],
         ),
         out_shape=jax.ShapeDtypeStruct(shape, F32),
         input_output_aliases=aliases,
         cost_estimate=pl.CostEstimate(flops=30_000_000_000, bytes_accessed=n_group * 44_000_000, transcendentals=0),
-        compiler_params=pltpu.CompilerParams(dimension_semantics=('arbitrary',), vmem_limit_bytes=48 * 2**20),
+        compiler_params=pltpu.CompilerParams(dimension_semantics=('arbitrary',), vmem_limit_bytes=56 * 2**20),
         name='place_rows',
     )(*args)
 
@@ -301,7 +342,9 @@
         own_off = tok_ids - base
         own_mask = (own_off >= 0) & (own_off < range_rows)
         peer_ids = lax.ppermute(tok_ids, 'emb', swap)
-        offsets = jnp.clip(jnp.concatenate([own_off, peer_ids - base]), 0, range_rows - 1)
+        pair_off = jnp.concatenate([own_off, peer_ids - base])
+        spread = (jnp.arange(pair_off.shape[0], dtype=jnp.int32) * 32) % range_rows
+        offsets = jnp.where((pair_off >= 0) & (pair_off < range_rows), pair_off, spread)
         served = run_fetch(tables, offsets)
         from_peer = lax.ppermute(served[:, tok_count:], 'emb', swap)
         fetched = jnp.where(own_mask[None, :, None], served[:, :tok_count], from_peer)
@@ -313,8 +356,12 @@
         all_off = jnp.where((all_off >= 0) & (all_off < range_rows), all_off, range_rows)
         keys = jnp.sort((all_off << idx_bits) | jnp.arange(n_all, dtype=jnp.int32))
         n_blocks = pl.cdiv(range_rows, OUT_ROWS)
+        pad = jnp.full((PLACE_UNROLL,), range_rows << idx_bits, jnp.int32)
         bounds = jnp.minimum(jnp.arange(n_blocks + 1, dtype=jnp.int32) * OUT_ROWS, range_rows)
         starts = jnp.sum((all_off[None, :] < bounds[:, None]).astype(jnp.int32), axis=1)
+
+        keys = jnp.concatenate([keys, pad])
+        keys, starts, fetched = lax.optimization_barrier((keys, starts, fetched))
 
         resid_out, xs, dg, gp = run_forward(resid_in, fetched, w_up, w_down, w_gate, w_proj)
 
@@ -322,6 +369,8 @@
         rows_list = [None] * n_layers
         for layer in reversed(range(n_layers)):
             cot, grad_rows = run_backward(layer, cot, xs, fetched, gp, dg, w_up, w_down, w_gate, w_proj)
+            if layer == 0:
+                grad_rows, rows_list[1] = lax.optimization_barrier((grad_rows, rows_list[1]))
             rows_list[layer] = lax.all_gather(grad_rows, ('dp', 'emb'), axis=0, tiled=True)
 
         d_tables = None

time: 767 us -> 716 us (0.934)
  Pallas kernels: 675 us -> 565 us
  waiting for transfers between devices: 3.83 us -> 99.6 us
  starting transfers between devices: 33.5 us -> 1.46 us
    all_gather x6, waiting for transfers between devices: 0.06 us -> 97 us  [device_body(): lax.all_gather(grad_rows, ('dp', 'emb'), axis=0, tiled=True)]
    pallas_call x8, Pallas kernels: 407 us -> 326 us  [the longest x6 208 us: run_backward(): pl.pallas_call(functools.partial(backward_body, n_tiles), grid=(n_tiles +...]
    ppermute x1, starting transfers between devices: 21.2 us -> 0.34 us  [device_body(): from_peer = lax.ppermute(served[:, tok_count:], 'emb', swap)]
    pallas_call x1, Pallas kernels: 225 us -> 206 us  [run_forward(): pl.pallas_call(functools.partial(forward_body, n_layers, n_tiles), grid=(...]
    all_gather x6, starting transfers between devices: 11.4 us -> 0.23 us  [device_body(): lax.all_gather(grad_rows, ('dp', 'emb'), axis=0, tiled=True)]
    pallas_call x1, Pallas kernels: 43.4 us -> 32.7 us  [run_fetch(): pl.pallas_call(functools.partial(fetch_body, n_layers, FETCH_TOK, n_steps...]
  transfers between devices with their start and end apart: 8 -> 8, of which waited for: 2 -> 5; matrix products, arithmetic and copies ran while one was open for 1% -> 1% of each run, Pallas kernels for 37% -> 13%
where the time goes in v2:
time: 716 us; the launch traced here: 709 us
  Pallas kernels  565 us (79%)
  waiting for transfers between devices  99.6 us (14%)
  between operations  14.4 us (2%)
  blocking collectives  13.1 us (2%)
  other arithmetic  12 us (2%)
    pallas_call x6, Pallas kernels, run_backward(): pl.pallas_call(functools.partial(backward_body, n_tiles), grid=(n_tiles +...  208 us
    pallas_call x1, Pallas kernels, run_forward(): pl.pallas_call(functools.partial(forward_body, n_layers, n_tiles), grid=(...  206 us
    pallas_call x2, Pallas kernels, run_place(): pl.pallas_call(functools.partial(place_body, group, n_group, idx_bits, n_...  118 us
    all_gather x6, waiting for transfers between devices, device_body(): lax.all_gather(grad_rows, ('dp', 'emb'), axis=0, tiled=True)  97 us
    pallas_call x1, Pallas kernels, run_fetch(): pl.pallas_call(functools.partial(fetch_body, n_layers, FETCH_TOK, n_steps...  32.7 us
  transfers between devices with their start and end apart: 8, of which 5 were waited for; matrix products, arithmetic and copies ran while one was open for 1% of the time, Pallas kernels for 13%

profile of v2, /device:TPU:0, one launch (start us, length us, event | category | flops | bytes accessed | tf_op | source)
XLA Modules:
  0.0 708.7 jit_solution(44710287410052065)
XLA Ops:
  7.2 0.0 all-gather.7.cloned.1.call-start
  7.2 0.9 collective-permute-start
  8.1 0.7 compare_and_fusion
  8.8 0.1 collective-permute-done
  8.9 0.6 fusion.off_ref
  9.5 0.0 copy-start.1
  9.5 32.7 %fetch_rows.1 = bf16[6,2048,128]{2,1,0:T(8,128)(2,1)} custom-call(s32[2048]{0:T(1024)} %fusion.off_ref, bf16[6,75968,128]{2,1,0:T(8,128)(2,1)} %table_ref.1), custom_call_target="tpu_custom_call" | custom-call | flops 2000000000 | bytes 30000000 | tf_op jit(solution)/shard_map/fetch_rows/pallas_call | solution.py:238
  42.2 0.0 copy-start
  42.2 2.8 slice.9
  45.1 0.3 collective-permute-start.1
  45.4 0.0 copy-done.1
  45.4 13.1 %all_gather.21 = s32[8192]{0:T(1024)S(1)} all-gather(s32[1024]{0:T(1024)S(1)} %copy-done.1), channel_id=1, replica_groups=mesh['dp'=4,'emb'=2] {'dp','emb'}, dimensions={0}, use_global_device_ids=true | all-gather | bytes 36864 | tf_op jit(solution)/shard_map/all_gather | solution.py:352
  58.5 6.8 sort.15
  65.3 0.6 concatenate.6.keys_ref
  65.9 1.1 convert_reduce_fusion.starts_ref
  67.0 0.0 collective-permute-done.1
  67.0 0.0 copy-done
  67.0 2.8 slice_select_fusion.e_ref
  69.8 206.2 %forward.1 = (bf16[1024,896]{1,0:T(8,128)(2,1)}, bf16[6,1024,896]{2,1,0:T(8,128)(2,1)}, f32[6,19,1024,256]{3,2,1,0:T(8,128)}, f32[6,1024,128]{2,1,0:T(8,128)}) custom-call(bf16[1024,896]{1,0:T(8,128)(2,1)} %x_ref.1, bf16[6,1024,128]{2,1,0:T(8,128)(2,1)} %slice_select_fusion.e_ref, bf16[6,896,4864]{2,1,0:T(8,128)(2,1)} %wu_ref.13, ...), custom_call_target="tpu_custom_call" | custom-call | flops 107105746944 | bytes 240000000 | tf_op jit(solution)/shard_map/forward/pallas_call | solution.py:97
  276.0 34.5 %backward.6 = (bf16[1024,896]{1,0:T(8,128)(2,1)}, f32[1024,128]{1,0:T(8,128)}) custom-call(bf16[1024,896]{1,0:T(8,128)(2,1)} %c_ref.1, bf16[6,1024,896]{2,1,0:T(8,128)(2,1)} %get-tuple-element.29.xs_ref, bf16[6,1024,128]{2,1,0:T(8,128)(2,1)} %slice_select_fusion.e_ref, f32[6,1024,128]{2,1,0:T(8,128)} %get-tuple-element.30.gp_ref, ...), custom_call_target="tpu_custom_call" | custom-call | flops 17850957824 | bytes 40000000 | tf_op jit(solution)/shard_map/backward/pallas_call | solution.py:170
  310.5 34.8 %backward.7 = (bf16[1024,896]{1,0:T(8,128)(2,1)}, f32[1024,128]{1,0:T(8,128)}) custom-call(bf16[1024,896]{1,0:T(8,128)(2,1)} %get-tuple-element.32.c_ref, bf16[6,1024,896]{2,1,0:T(8,128)(2,1)} %get-tuple-element.29.xs_ref, bf16[6,1024,128]{2,1,0:T(8,128)(2,1)} %slice_select_fusion.e_ref, f32[6,1024,128]{2,1,0:T(8,128)} %get-tuple-element.30.gp_ref, ...), custom_call_target="tpu_custom_call" | custom-call | flops 17850957824 | bytes 40000000 | tf_op jit(solution)/shard_map/backward/pallas_call | solution.py:170
  345.3 34.5 %backward.8 = (bf16[1024,896]{1,0:T(8,128)(2,1)}, f32[1024,128]{1,0:T(8,128)}) custom-call(bf16[1024,896]{1,0:T(8,128)(2,1)} %get-tuple-element.33.c_ref, bf16[6,1024,896]{2,1,0:T(8,128)(2,1)} %get-tuple-element.29.xs_ref, bf16[6,1024,128]{2,1,0:T(8,128)(2,1)} %slice_select_fusion.e_ref, f32[6,1024,128]{2,1,0:T(8,128)} %get-tuple-element.30.gp_ref, ...), custom_call_target="tpu_custom_call" | custom-call | flops 17850957824 | bytes 40000000 | tf_op jit(solution)/shard_map/backward/pallas_call | solution.py:170
  379.8 35.0 %backward.9 = (bf16[1024,896]{1,0:T(8,128)(2,1)}, f32[1024,128]{1,0:T(8,128)}) custom-call(bf16[1024,896]{1,0:T(8,128)(2,1)} %get-tuple-element.34.c_ref, bf16[6,1024,896]{2,1,0:T(8,128)(2,1)} %get-tuple-element.29.xs_ref, bf16[6,1024,128]{2,1,0:T(8,128)(2,1)} %slice_select_fusion.e_ref, f32[6,1024,128]{2,1,0:T(8,128)} %get-tuple-element.30.gp_ref, ...), custom_call_target="tpu_custom_call" | custom-call | flops 17850957824 | bytes 40000000 | tf_op jit(solution)/shard_map/backward/pallas_call | solution.py:170
  414.8 34.5 %backward.10 = (bf16[1024,896]{1,0:T(8,128)(2,1)}, f32[1024,128]{1,0:T(8,128)}) custom-call(bf16[1024,896]{1,0:T(8,128)(2,1)} %get-tuple-element.35.c_ref, bf16[6,1024,896]{2,1,0:T(8,128)(2,1)} %get-tuple-element.29.xs_ref, bf16[6,1024,128]{2,1,0:T(8,128)(2,1)} %slice_select_fusion.e_ref, f32[6,1024,128]{2,1,0:T(8,128)} %get-tuple-element.30.gp_ref, ...), custom_call_target="tpu_custom_call" | custom-call | flops 17850957824 | bytes 40000000 | tf_op jit(solution)/shard_map/backward/pallas_call | solution.py:170
  449.2 0.0 all-gather.7.cloned.1.call-update
  449.3 0.0 all-gather.17.cloned.1.call-start
  449.3 0.7 all-gather.17.cloned.1.call-update
  450.0 0.0 all-gather.15.cloned.1.call-start
  450.1 0.7 all-gather.15.cloned.1.call-update
  450.7 0.0 all-gather.13.cloned.1.call-start
  450.8 0.5 all-gather.13.cloned.1.call-update
  451.3 0.0 all-gather.11.cloned.1.call-start
  451.4 0.5 all-gather.11.cloned.1.call-update
  451.9 0.0 all-gather.9.cloned.1.call-start
  452.0 34.7 %backward.11 = (bf16[1024,896]{1,0:T(8,128)(2,1)}, f32[1024,128]{1,0:T(8,128)}) custom-call(bf16[1024,896]{1,0:T(8,128)(2,1)} %get-tuple-element.36.c_ref, bf16[6,1024,896]{2,1,0:T(8,128)(2,1)} %get-tuple-element.29.xs_ref, bf16[6,1024,128]{2,1,0:T(8,128)(2,1)} %slice_select_fusion.e_ref, f32[6,1024,128]{2,1,0:T(8,128)} %get-tuple-element.30.gp_ref, ...), custom_call_target="tpu_custom_call" | custom-call | flops 17850957824 | bytes 40000000 | tf_op jit(solution)/shard_map/backward/pallas_call | solution.py:170
  486.7 0.0 all-gather.7.cloned.1.call-done.refs_1_
  486.7 0.0 all-gather.9.cloned.1.call-update
  486.7 26.1 %all-gather.17.cloned.1.call-done.refs_2_ = f32[8192,128]{1,0:T(8,128)} async-done(((f32[1024,128]{1,0:T(8,128)}), f32[8192,128]{1,0:T(8,128)}) %all-gather.17.cloned.1.call-update) | async-done | bytes 4194320 | tf_op jit(solution)/shard_map/all_gather | solution.py:374
  512.8 32.6 %all-gather.15.cloned.1.call-done.refs_1_ = f32[8192,128]{1,0:T(8,128)} async-done(((f32[1024,128]{1,0:T(8,128)}), f32[8192,128]{1,0:T(8,128)}) %all-gather.15.cloned.1.call-update) | async-done | bytes 4194320 | tf_op jit(solution)/shard_map/all_gather | solution.py:374
  545.4 32.4 %all-gather.13.cloned.1.call-done.refs_0_ = f32[8192,128]{1,0:T(8,128)} async-done(((f32[1024,128]{1,0:T(8,128)}), f32[8192,128]{1,0:T(8,128)}) %all-gather.13.cloned.1.call-update) | async-done | bytes 4194320 | tf_op jit(solution)/shard_map/all_gather | solution.py:374
  577.8 58.9 %place_rows.2.refs_3_ = f32[6,75968,128]{2,1,0:T(8,128)} custom-call(s32[76]{0:T(128)} %convert_reduce_fusion.starts_ref, s32[8200]{0:T(1024)} %concatenate.6.keys_ref, f32[8192,128]{1,0:T(8,128)} %all-gather.13.cloned.1.call-done.refs_0_, f32[8192,128]{1,0:T(8,128)} %all-gather.15.cloned.1.call-done.refs_1_, f32[8192,128]{1,0:T(8,128)} %all-gather.17.cloned.1.call-done.refs_2_), custom_call_target="tpu_custom_call" | custom-call | flops 30000001024 | bytes 132000000 | tf_op jit(solution)/shard_map/place_rows/pallas_call | solution.py:312
  636.8 0.0 all-gather.11.cloned.1.call-done.refs_2_
  636.8 5.9 all-gather.9.cloned.1.call-done.refs_0_
  642.7 58.9 %place_rows.3 = f32[6,75968,128]{2,1,0:T(8,128)} custom-call(s32[76]{0:T(128)} %convert_reduce_fusion.starts_ref, s32[8200]{0:T(1024)} %concatenate.6.keys_ref, f32[8192,128]{1,0:T(8,128)} %all-gather.9.cloned.1.call-done.refs_0_, f32[8192,128]{1,0:T(8,128)} %all-gather.7.cloned.1.call-done.refs_1_, ...), custom_call_target="tpu_custom_call", output_to_operand_aliasing={{}: (5, {})} | custom-call | flops 30000001024 | bytes 132000000 | tf_op jit(solution)/shard_map/place_rows/pallas_call | solution.py:312
  (4 shorter events, 0.0 us)
Async XLA Ops:
  7.2 479.5 %all-gather.7.cloned.1.call-start = ((), (), s32[]{:S(2)}) async-start(), calls=%async_computation | async-start | bytes 4718592 | tf_op jit(solution)/shard_map/all_gather | solution.py:374
  7.2 1.7 collective-permute-start
  9.5 35.9 %copy-start.1 = (s32[1024]{0:T(1024)S(1)}, s32[1024]{0:T(1024)}, u32[]{:S(2)}) copy-start(s32[1024]{0:T(1024)} %param.8) | copy-start | bytes 12292
  42.2 24.8 %copy-start = (bf16[6,2048,128]{2,1,0:T(8,128)(2,1)S(1)}, bf16[6,2048,128]{2,1,0:T(8,128)(2,1)}, u32[]{:S(2)}) copy-start(bf16[6,2048,128]{2,1,0:T(8,128)(2,1)} %fetch_rows.1) | copy-start | bytes 9437188
  45.1 21.9 %collective-permute-start.1 = (bf16[6,1024,128]{2,1,0:T(8,128)(2,1)}, bf16[6,1024,128]{2,1,0:T(8,128)(2,1)}, u32[]{:S(2)}, u32[]{:S(2)}) collective-permute-start(bf16[6,1024,128]{2,1,0:T(8,128)(2,1)} %slice.9), channel_id=1, source_target_pairs={{0,1},{1,0},{2,3},{3,2},{4,5},{5,4},{6,7},{7,6}} | collective-permute-start | bytes 4718600 | tf_op jit(solution)/shard_map/ppermute | solution.py:349
  449.3 63.5 %all-gather.17.cloned.1.call-start = ((), (), s32[]{:S(2)}) async-start(), calls=%async_computation.5 | async-start | bytes 4718592 | tf_op jit(solution)/shard_map/all_gather | solution.py:374
  450.0 95.3 %all-gather.15.cloned.1.call-start = ((), (), s32[]{:S(2)}) async-start(), calls=%async_computation.4 | async-start | bytes 4718592 | tf_op jit(solution)/shard_map/all_gather | solution.py:374
  450.7 127.1 %all-gather.13.cloned.1.call-start = ((), (), s32[]{:S(2)}) async-start(), calls=%async_computation.3 | async-start | bytes 4718592 | tf_op jit(solution)/shard_map/all_gather | solution.py:374
  451.3 185.5 %all-gather.11.cloned.1.call-start = ((), (), s32[]{:S(2)}) async-start(), calls=%async_computation.2 | async-start | bytes 4718592 | tf_op jit(solution)/shard_map/all_gather | solution.py:374
  451.9 190.8 %all-gather.9.cloned.1.call-start = ((), (), s32[]{:S(2)}) async-start(), calls=%async_computation.1 | async-start | bytes 4718592 | tf_op jit(solution)/shard_map/all_gather | solution.py:374
Sparse Core Ops, SparseCore 0:
  449.4 30.7 all-gather.6
  482.0 30.7 all-gather.16
  514.6 30.7 all-gather.14
  547.0 30.7 all-gather.12
  579.5 30.7 all-gather.10
  611.9 30.7 all-gather.8

commit v3 on v2

--- a/solution.py
+++ b/solution.py
@@ -368,6 +368,8 @@
         cot = cot_out
         rows_list = [None] * n_layers
         for layer in reversed(range(n_layers)):
+            if layer + 2 < n_layers:
+                cot, rows_list[layer + 2] = lax.optimization_barrier((cot, rows_list[layer + 2]))
             cot, grad_rows = run_backward(layer, cot, xs, fetched, gp, dg, w_up, w_down, w_gate, w_proj)
             if layer == 0:
                 grad_rows, rows_list[1] = lax.optimization_barrier((grad_rows, rows_list[1]))

time: 716 us -> 617 us (0.86)
  waiting for transfers between devices: 99.6 us -> 0.33 us
    all_gather x6, waiting for transfers between devices: 97 us -> 0.1 us  [device_body(): lax.all_gather(grad_rows, ('dp', 'emb'), axis=0, tiled=True)]
  transfers between devices with their start and end apart: 8 -> 8, of which waited for: 5 -> 1; matrix products, arithmetic and copies ran while one was open for 1% -> 1% of each run, Pallas kernels for 13% -> 38%
where the time goes in v3:
time: 617 us; the launch traced here: 609 us
  Pallas kernels  565 us (92%)
  between operations  14.4 us (2%)
  blocking collectives  13.1 us (2%)
  other arithmetic  12 us (2%)
    pallas_call x6, Pallas kernels, run_backward(): pl.pallas_call(functools.partial(backward_body, n_tiles), grid=(n_tiles +...  208 us
    pallas_call x1, Pallas kernels, run_forward(): pl.pallas_call(functools.partial(forward_body, n_layers, n_tiles), grid=(...  206 us
    pallas_call x2, Pallas kernels, run_place(): pl.pallas_call(functools.partial(place_body, group, n_group, idx_bits, n_...  118 us
    pallas_call x1, Pallas kernels, run_fetch(): pl.pallas_call(functools.partial(fetch_body, n_layers, FETCH_TOK, n_steps...  32.7 us
    all_gather x1, blocking collectives, device_body(): all_ids = lax.all_gather(tok_ids, ('dp', 'emb'), axis=0, tiled=True)  13.1 us
  transfers between devices with their start and end apart: 8, of which 1 were waited for; matrix products, arithmetic and copies ran while one was open for 1% of the time, Pallas kernels for 38%

profile of v3, /device:TPU:0, one launch (start us, length us, event | category | flops | bytes accessed | tf_op | source)
XLA Modules:
  0.0 609.4 jit_solution(12784138871794196101)
XLA Ops:
  7.2 0.0 all-gather.7.cloned.1.call-start
  7.2 0.9 collective-permute-start
  8.1 0.7 compare_and_fusion
  8.8 0.1 collective-permute-done
  8.9 0.6 fusion.off_ref
  9.5 0.0 copy-start.1
  9.5 32.7 %fetch_rows.1 = bf16[6,2048,128]{2,1,0:T(8,128)(2,1)} custom-call(s32[2048]{0:T(1024)} %fusion.off_ref, bf16[6,75968,128]{2,1,0:T(8,128)(2,1)} %table_ref.1), custom_call_target="tpu_custom_call" | custom-call | flops 2000000000 | bytes 30000000 | tf_op jit(solution)/shard_map/fetch_rows/pallas_call | solution.py:238
  42.2 0.0 copy-start
  42.2 2.8 slice.9
  45.1 0.3 collective-permute-start.1
  45.4 0.0 copy-done.1
  45.4 13.1 %all_gather.21 = s32[8192]{0:T(1024)S(1)} all-gather(s32[1024]{0:T(1024)S(1)} %copy-done.1), channel_id=1, replica_groups=mesh['dp'=4,'emb'=2] {'dp','emb'}, dimensions={0}, use_global_device_ids=true | all-gather | bytes 36864 | tf_op jit(solution)/shard_map/all_gather | solution.py:352
  58.5 6.8 %sort.15 = (s32[8192]{0:T(1024)S(1)}, s32[8192]{0:T(1024)}) sort(s32[8192]{0:T(1024)S(1)} %get-tuple-element.63, s32[8192]{0:T(1024)S(1)} %iota.15), dimensions={0}, to_apply=%region_0.1 | sort | flops 106496 | bytes 131072 | tf_op jit(solution)/shard_map/jit(sort)/sort | solution.py:357
  65.3 0.6 concatenate.6.keys_ref
  65.9 1.0 convert_reduce_fusion.starts_ref
  67.0 0.0 collective-permute-done.1
  67.0 0.0 copy-done
  67.0 2.8 slice_select_fusion.e_ref
  69.8 206.2 %forward.1 = (bf16[1024,896]{1,0:T(8,128)(2,1)}, bf16[6,1024,896]{2,1,0:T(8,128)(2,1)}, f32[6,19,1024,256]{3,2,1,0:T(8,128)}, f32[6,1024,128]{2,1,0:T(8,128)}) custom-call(bf16[1024,896]{1,0:T(8,128)(2,1)} %x_ref.1, bf16[6,1024,128]{2,1,0:T(8,128)(2,1)} %slice_select_fusion.e_ref, bf16[6,896,4864]{2,1,0:T(8,128)(2,1)} %wu_ref.13, ...), custom_call_target="tpu_custom_call" | custom-call | flops 107105746944 | bytes 240000000 | tf_op jit(solution)/shard_map/forward/pallas_call | solution.py:97
  275.9 34.5 %backward.6 = (bf16[1024,896]{1,0:T(8,128)(2,1)}, f32[1024,128]{1,0:T(8,128)}) custom-call(bf16[1024,896]{1,0:T(8,128)(2,1)} %c_ref.1, bf16[6,1024,896]{2,1,0:T(8,128)(2,1)} %get-tuple-element.37.xs_ref, bf16[6,1024,128]{2,1,0:T(8,128)(2,1)} %slice_select_fusion.e_ref, f32[6,1024,128]{2,1,0:T(8,128)} %get-tuple-element.38.gp_ref, ...), custom_call_target="tpu_custom_call" | custom-call | flops 17850957824 | bytes 40000000 | tf_op jit(solution)/shard_map/backward/pallas_call | solution.py:170
  310.5 0.0 all-gather.7.cloned.1.call-update
  310.5 0.0 all-gather.9.cloned.1.call-start
  310.5 34.7 %backward.7 = (bf16[1024,896]{1,0:T(8,128)(2,1)}, f32[1024,128]{1,0:T(8,128)}) custom-call(bf16[1024,896]{1,0:T(8,128)(2,1)} %get-tuple-element.40.c_ref, bf16[6,1024,896]{2,1,0:T(8,128)(2,1)} %get-tuple-element.37.xs_ref, bf16[6,1024,128]{2,1,0:T(8,128)(2,1)} %slice_select_fusion.e_ref, f32[6,1024,128]{2,1,0:T(8,128)} %get-tuple-element.38.gp_ref, ...), custom_call_target="tpu_custom_call" | custom-call | flops 17850957824 | bytes 40000000 | tf_op jit(solution)/shard_map/backward/pallas_call | solution.py:170
  345.2 0.0 all-gather.9.cloned.1.call-update
  345.3 0.0 all-gather.11.cloned.1.call-start
  345.3 0.0 all-gather.7.cloned.1.call-done.refs_2_
  345.3 34.6 %backward.8 = (bf16[1024,896]{1,0:T(8,128)(2,1)}, f32[1024,128]{1,0:T(8,128)}) custom-call(bf16[1024,896]{1,0:T(8,128)(2,1)} %get-tuple-element.43.c_ref, bf16[6,1024,896]{2,1,0:T(8,128)(2,1)} %get-tuple-element.37.xs_ref, bf16[6,1024,128]{2,1,0:T(8,128)(2,1)} %slice_select_fusion.e_ref, f32[6,1024,128]{2,1,0:T(8,128)} %get-tuple-element.38.gp_ref, ...), custom_call_target="tpu_custom_call" | custom-call | flops 17850957824 | bytes 40000000 | tf_op jit(solution)/shard_map/backward/pallas_call | solution.py:170
  380.0 0.0 all-gather.11.cloned.1.call-update
  380.0 0.0 all-gather.13.cloned.1.call-start
  380.0 0.0 all-gather.9.cloned.1.call-done.refs_1_
  380.1 34.9 %backward.9 = (bf16[1024,896]{1,0:T(8,128)(2,1)}, f32[1024,128]{1,0:T(8,128)}) custom-call(bf16[1024,896]{1,0:T(8,128)(2,1)} %get-tuple-element.46.c_ref, bf16[6,1024,896]{2,1,0:T(8,128)(2,1)} %get-tuple-element.37.xs_ref, bf16[6,1024,128]{2,1,0:T(8,128)(2,1)} %slice_select_fusion.e_ref, f32[6,1024,128]{2,1,0:T(8,128)} %get-tuple-element.38.gp_ref, ...), custom_call_target="tpu_custom_call" | custom-call | flops 17850957824 | bytes 40000000 | tf_op jit(solution)/shard_map/backward/pallas_call | solution.py:170
  415.0 0.0 all-gather.13.cloned.1.call-update
  415.0 0.0 all-gather.15.cloned.1.call-start
  415.0 0.0 all-gather.11.cloned.1.call-done.refs_0_
  415.1 34.5 %backward.10 = (bf16[1024,896]{1,0:T(8,128)(2,1)}, f32[1024,128]{1,0:T(8,128)}) custom-call(bf16[1024,896]{1,0:T(8,128)(2,1)} %get-tuple-element.49.c_ref, bf16[6,1024,896]{2,1,0:T(8,128)(2,1)} %get-tuple-element.37.xs_ref, bf16[6,1024,128]{2,1,0:T(8,128)(2,1)} %slice_select_fusion.e_ref, f32[6,1024,128]{2,1,0:T(8,128)} %get-tuple-element.38.gp_ref, ...), custom_call_target="tpu_custom_call" | custom-call | flops 17850957824 | bytes 40000000 | tf_op jit(solution)/shard_map/backward/pallas_call | solution.py:170
  449.5 0.0 all-gather.15.cloned.1.call-update
  449.6 0.0 all-gather.17.cloned.1.call-start
  449.6 0.0 all-gather.13.cloned.1.call-done.refs_2_
  449.6 34.7 %backward.11 = (bf16[1024,896]{1,0:T(8,128)(2,1)}, f32[1024,128]{1,0:T(8,128)}) custom-call(bf16[1024,896]{1,0:T(8,128)(2,1)} %get-tuple-element.52.c_ref, bf16[6,1024,896]{2,1,0:T(8,128)(2,1)} %get-tuple-element.37.xs_ref, bf16[6,1024,128]{2,1,0:T(8,128)(2,1)} %slice_select_fusion.e_ref, f32[6,1024,128]{2,1,0:T(8,128)} %get-tuple-element.38.gp_ref, ...), custom_call_target="tpu_custom_call" | custom-call | flops 17850957824 | bytes 40000000 | tf_op jit(solution)/shard_map/backward/pallas_call | solution.py:170
  484.3 0.0 all-gather.15.cloned.1.call-done.refs_1_
  484.3 0.0 all-gather.17.cloned.1.call-update
  484.4 59.0 %place_rows.2.refs_3_ = f32[6,75968,128]{2,1,0:T(8,128)} custom-call(s32[76]{0:T(128)} %convert_reduce_fusion.starts_ref, s32[8200]{0:T(1024)} %concatenate.6.keys_ref, f32[8192,128]{1,0:T(8,128)} %all-gather.11.cloned.1.call-done.refs_0_, f32[8192,128]{1,0:T(8,128)} %all-gather.9.cloned.1.call-done.refs_1_, f32[8192,128]{1,0:T(8,128)} %all-gather.7.cloned.1.call-done.refs_2_), custom_call_target="tpu_custom_call" | custom-call | flops 30000001024 | bytes 132000000 | tf_op jit(solution)/shard_map/place_rows/pallas_call | solution.py:312
  543.3 0.0 all-gather.17.cloned.1.call-done.refs_0_
  543.4 59.0 %place_rows.3 = f32[6,75968,128]{2,1,0:T(8,128)} custom-call(s32[76]{0:T(128)} %convert_reduce_fusion.starts_ref, s32[8200]{0:T(1024)} %concatenate.6.keys_ref, f32[8192,128]{1,0:T(8,128)} %all-gather.17.cloned.1.call-done.refs_0_, f32[8192,128]{1,0:T(8,128)} %all-gather.15.cloned.1.call-done.refs_1_, ...), custom_call_target="tpu_custom_call", output_to_operand_aliasing={{}: (5, {})} | custom-call | flops 30000001024 | bytes 132000000 | tf_op jit(solution)/shard_map/place_rows/pallas_call | solution.py:312
  (4 shorter events, 0.0 us)
Async XLA Ops:
  7.2 338.2 %all-gather.7.cloned.1.call-start = ((), (), s32[]{:S(2)}) async-start(), calls=%async_computation | async-start | bytes 4718592 | tf_op jit(solution)/shard_map/all_gather | solution.py:376
  7.2 1.7 collective-permute-start
  9.5 35.9 %copy-start.1 = (s32[1024]{0:T(1024)S(1)}, s32[1024]{0:T(1024)}, u32[]{:S(2)}) copy-start(s32[1024]{0:T(1024)} %param.8) | copy-start | bytes 12292
  42.2 24.7 %copy-start = (bf16[6,2048,128]{2,1,0:T(8,128)(2,1)S(1)}, bf16[6,2048,128]{2,1,0:T(8,128)(2,1)}, u32[]{:S(2)}) copy-start(bf16[6,2048,128]{2,1,0:T(8,128)(2,1)} %fetch_rows.1) | copy-start | bytes 9437188
  45.1 21.9 %collective-permute-start.1 = (bf16[6,1024,128]{2,1,0:T(8,128)(2,1)}, bf16[6,1024,128]{2,1,0:T(8,128)(2,1)}, u32[]{:S(2)}, u32[]{:S(2)}) collective-permute-start(bf16[6,1024,128]{2,1,0:T(8,128)(2,1)} %slice.9), channel_id=1, source_target_pairs={{0,1},{1,0},{2,3},{3,2},{4,5},{5,4},{6,7},{7,6}} | collective-permute-start | bytes 4718600 | tf_op jit(solution)/shard_map/ppermute | solution.py:349
  310.5 69.6 %all-gather.9.cloned.1.call-start = ((), (), s32[]{:S(2)}) async-start(), calls=%async_computation.1 | async-start | bytes 4718592 | tf_op jit(solution)/shard_map/all_gather | solution.py:376
  345.3 69.8 %all-gather.11.cloned.1.call-start = ((), (), s32[]{:S(2)}) async-start(), calls=%async_computation.2 | async-start | bytes 4718592 | tf_op jit(solution)/shard_map/all_gather | solution.py:376
  380.0 69.7 %all-gather.13.cloned.1.call-start = ((), (), s32[]{:S(2)}) async-start(), calls=%async_computation.3 | async-start | bytes 4718592 | tf_op jit(solution)/shard_map/all_gather | solution.py:376
  415.0 69.3 %all-gather.15.cloned.1.call-start = ((), (), s32[]{:S(2)}) async-start(), calls=%async_computation.4 | async-start | bytes 4718592 | tf_op jit(solution)/shard_map/all_gather | solution.py:376
  449.6 93.8 %all-gather.17.cloned.1.call-start = ((), (), s32[]{:S(2)}) async-start(), calls=%async_computation.5 | async-start | bytes 4718592 | tf_op jit(solution)/shard_map/all_gather | solution.py:376
Sparse Core Ops, SparseCore 0:
  310.6 30.7 all-gather.6
  345.4 30.7 all-gather.8
  380.1 30.7 all-gather.10
  415.1 30.7 all-gather.12
  449.7 30.7 all-gather.14
  484.5 30.7 all-gather.16

commit v4 on v3

--- a/solution.py
+++ b/solution.py
@@ -11,11 +11,13 @@
 GELU_K = 0.7978845608028654
 GELU_A = 0.044715
 F_TILE = 256
+RING = 6
+SLOPE_RING = 4
 FWD_CHUNK = 256
 BWD_CHUNK = 1024
 OUT_ROWS = 1024
 PLACE_UNROLL = 8
-PLACE_BUFS = 4
+PLACE_BUFS = 12
 FETCH_TOK = 128
 F32 = jnp.float32
 BF16 = jnp.bfloat16
@@ -41,124 +43,202 @@
     return [pl.ds(r, min(size, rows)) for r in range(0, rows, size)]
 
 
-def forward_body(n_layers, n_tiles, x_ref, e_ref, wu_ref, wd_ref, wg_ref, wp_ref, out_ref, xs_ref, dg_ref, gp_ref, x_s, u_s, h_s, acc_s):
-    layer, tile = pl.program_id(0), pl.program_id(1)
+def weight_copy(src, buf, sems, layer, tile, index, by_rows):
+    span = pl.ds(pl.multiple_of(tile * F_TILE, F_TILE), F_TILE)
+    part = src.at[layer, span, :] if by_rows else src.at[layer, :, span]
+    slot = index % RING
+    return pltpu.make_async_copy(part, buf.at[slot], sems.at[slot])
+
+
+def forward_body(n_layers, n_tiles, x_ref, e_ref, wu_ref, wd_ref, wg_ref, wp_ref, out_ref, xs_ref, dg_ref, gp_ref, x_s, u_s, h_s, acc_s, wu_s, wd_s, dg_s, wu_sem, wd_sem, dg_sem):
+    layer = pl.program_id(0)
     chunks = row_chunks(x_s.shape[0], FWD_CHUNK)
-
-    def up_half(r):
-        act, slope = gelu_pair(dot_nn(u_s[r, :], wu_ref[0]))
-        dg_ref[0, 0, r, :] = slope
+    total = n_layers * n_tiles
+    first = layer * n_tiles
+
+    def up_copy(i):
+        return weight_copy(wu_ref, wu_s, wu_sem, i // n_tiles, i % n_tiles, i, False)
+
+    def down_copy(i):
+        return weight_copy(wd_ref, wd_s, wd_sem, i // n_tiles, i % n_tiles, i, True)
+
+    def slope_copy(i):
+        return pltpu.make_async_copy(dg_s.at[i % SLOPE_RING], dg_ref.at[i // n_tiles, i % n_tiles], dg_sem.at[i % SLOPE_RING])
+
+    def enter(i):
+        @pl.when(i + RING - 1 < total)
+        def _():
+            up_copy(i + RING - 1).start()
+
+        @pl.when(i + RING - 2 < total)
+        def _():
+            down_copy(i + RING - 2).start()
+
+        @pl.when(i + 1 < total)
+        def _():
+            up_copy(i + 1).wait()
+
+        down_copy(i).wait()
+
+        @pl.when(i >= SLOPE_RING)
+        def _():
+            slope_copy(i - SLOPE_RING).wait()
+
+    def up_half(i, r):
+        act, slope = gelu_pair(dot_nn(u_s[r, :], wu_s[i % RING]))
+        dg_s[i % SLOPE_RING, r, :] = slope
         h_s[r, :] = act.astype(BF16)
 
-    def down_half(r):
-        acc_s[r, :] += dot_nn(h_s[r, :], wd_ref[0])
-
-    @pl.when((layer == 0) & (tile == 0))
-    def _():
+    @pl.when(layer == 0)
+    def _():
+        for i in range(min(RING - 1, total)):
+            up_copy(i).start()
+            if i < RING - 2:
+                down_copy(i).start()
         x_s[...] = x_ref[...]
-
-    @pl.when(tile == 0)
-    def _():
+        up_copy(0).wait()
+
+    enter(first)
+    for r in chunks:
+        x_bf = x_s[r, :]
+        xs_ref[0, r, :] = x_bf
+        x_f = x_bf.astype(F32)
+        u = (x_f * lax.rsqrt(jnp.mean(x_f * x_f, axis=-1, keepdims=True) + NORM_EPS)).astype(BF16)
+        u_s[r, :] = u
+        gate_pre = dot_nn(u, wg_ref[0])
+        gp_ref[0, r, :] = gate_pre
+        gate_act, _ = gelu_pair(gate_pre)
+        mixed = (gate_act * e_ref[0, r, :].astype(F32)).astype(BF16)
+        acc_s[r, :] = x_f + dot_nn(mixed, wp_ref[0])
+        up_half(first, r)
+    slope_copy(first).start()
+
+    def tile_step(tile, carry):
+        i = first + tile
+        enter(i)
         for r in chunks:
-            x_bf = x_s[r, :]
-            xs_ref[0, r, :] = x_bf
-            x_f = x_bf.astype(F32)
-            u = (x_f * lax.rsqrt(jnp.mean(x_f * x_f, axis=-1, keepdims=True) + NORM_EPS)).astype(BF16)
-            u_s[r, :] = u
-            gate_pre = dot_nn(u, wg_ref[0])
-            gp_ref[0, r, :] = gate_pre
-            gate_act, _ = gelu_pair(gate_pre)
-            mixed = (gate_act * e_ref[0, r, :].astype(F32)).astype(BF16)
-            acc_s[r, :] = x_f + dot_nn(mixed, wp_ref[0])
-            up_half(r)
-
-    @pl.when((tile > 0) & (tile < n_tiles))
-    def _():
-        for r in chunks:
-            down_half(r)
-            up_half(r)
-
-    @pl.when(tile == n_tiles)
-    def _():
-        for r in chunks:
-            x_s[r, :] = (acc_s[r, :] + dot_nn(h_s[r, :], wd_ref[0])).astype(BF16)
-
-    @pl.when((tile == n_tiles) & (layer == n_layers - 1))
+            acc_s[r, :] += dot_nn(h_s[r, :], wd_s[(i - 1) % RING])
+            up_half(i, r)
+        slope_copy(i).start()
+        return carry
+
+    lax.fori_loop(1, n_tiles, tile_step, 0)
+    for r in chunks:
+        x_s[r, :] = (acc_s[r, :] + dot_nn(h_s[r, :], wd_s[(first + n_tiles - 1) % RING])).astype(BF16)
+
+    @pl.when(layer == n_layers - 1)
     def _():
         out_ref[...] = x_s[...]
+        for i in range(max(0, total - SLOPE_RING), total):
+            slope_copy(i).wait()
 
 
 def run_forward(resid_in, fetched, w_up, w_down, w_gate, w_proj):
     n_layers, d_model, ffn = w_up.shape
     rows, e_dim = resid_in.shape[0], w_gate.shape[2]
     n_tiles = ffn // F_TILE
-    whole = pl.BlockSpec((rows, d_model), lambda l, j: (0, 0))
-    per_layer = lambda *s: pl.BlockSpec((1,) + s, lambda l, j: (l, 0, 0))
+    whole = pl.BlockSpec((rows, d_model), lambda l: (0, 0))
+    in_hbm = pl.BlockSpec(memory_space=pl.ANY)
+    per_layer = lambda *s: pl.BlockSpec((1,) + s, lambda l: (l, 0, 0))
     return pl.pallas_call(
         functools.partial(forward_body, n_layers, n_tiles),
-        grid=(n_layers, n_tiles + 1),
-        in_specs=[
-            whole,
-            per_layer(rows, e_dim),
-            pl.BlockSpec((1, d_model, F_TILE), lambda l, j: (l, 0, jnp.minimum(j, n_tiles - 1))),
-            pl.BlockSpec((1, F_TILE, d_model), lambda l, j: (l, jnp.maximum(j - 1, 0), 0)),
-            per_layer(d_model, e_dim),
-            per_layer(e_dim, d_model),
-        ],
-        out_specs=[
-            whole,
-            per_layer(rows, d_model),
-            pl.BlockSpec((1, 1, rows, F_TILE), lambda l, j: (l, jnp.minimum(j, n_tiles - 1), 0, 0)),
-            per_layer(rows, e_dim),
-        ],
+        grid=(n_layers,),
+        in_specs=[whole, per_layer(rows, e_dim), in_hbm, in_hbm, per_layer(d_model, e_dim), per_layer(e_dim, d_model)],
+        out_specs=[whole, per_layer(rows, d_model), in_hbm, per_layer(rows, e_dim)],
         out_shape=[
             jax.ShapeDtypeStruct((rows, d_model), BF16),
             jax.ShapeDtypeStruct((n_layers, rows, d_model), BF16),
             jax.ShapeDtypeStruct((n_layers, n_tiles, rows, F_TILE), F32),
             jax.ShapeDtypeStruct((n_layers, rows, e_dim), F32),
         ],
-        scratch_shapes=[pltpu.VMEM((rows, d_model), BF16), pltpu.VMEM((rows, d_model), BF16), pltpu.VMEM((rows, F_TILE), BF16), pltpu.VMEM((rows, d_model), F32)],
+        scratch_shapes=[
+            pltpu.VMEM((rows, d_model), BF16),
+            pltpu.VMEM((rows, d_model), BF16),
+            pltpu.VMEM((rows, F_TILE), BF16),
+            pltpu.VMEM((rows, d_model), F32),
+            pltpu.VMEM((RING, d_model, F_TILE), BF16),
+            pltpu.VMEM((RING, F_TILE, d_model), BF16),
+            pltpu.VMEM((SLOPE_RING, rows, F_TILE), F32),
+            pltpu.SemaphoreType.DMA((RING,)),
+            pltpu.SemaphoreType.DMA((RING,)),
+            pltpu.SemaphoreType.DMA((SLOPE_RING,)),
+        ],
         cost_estimate=pl.CostEstimate(flops=4 * n_layers * rows * d_model * ffn, bytes_accessed=n_layers * 40_000_000, transcendentals=0),
-        compiler_params=pltpu.CompilerParams(dimension_semantics=('arbitrary', 'arbitrary'), vmem_limit_bytes=56 * 2**20),
+        compiler_params=pltpu.CompilerParams(dimension_semantics=('arbitrary',), vmem_limit_bytes=56 * 2**20),
         name='forward',
     )(resid_in, fetched, w_up, w_down, w_gate, w_proj)
 
 
-def backward_body(n_tiles, c_ref, xs_ref, e_ref, gp_ref, dg_ref, wu_ref, wd_ref, wg_ref, wp_ref, cot_ref, gr_ref, dng_s, du_s, acc_s):
-    tile = pl.program_id(0)
+def backward_body(layer, n_tiles, c_ref, xs_ref, e_ref, gp_ref, dg_ref, wu_ref, wd_ref, wg_ref, wp_ref, cot_ref, gr_ref, xs_s, dng_s, du_s, acc_s, wu_s, wd_s, dg_s, wu_sem, wd_sem, dg_sem, xs_sem):
     chunks = row_chunks(c_ref.shape[0], BWD_CHUNK)
 
-    def hidden_half(r):
-        d_hidden = dot_nt(c_ref[r, :], wd_ref[0]).astype(BF16).astype(F32)
-        du_s[r, :] = (d_hidden * dg_ref[0, 0, r, :]).astype(BF16)
-
-    @pl.when(tile == 0)
-    def _():
+    def up_copy(i):
+        return weight_copy(wu_ref, wu_s, wu_sem, layer, i, i, False)
+
+    def down_copy(i):
+        return weight_copy(wd_ref, wd_s, wd_sem, layer, i, i, True)
+
+    def slope_copy(i):
+        return pltpu.make_async_copy(dg_ref.at[layer, i], dg_s.at[i % RING], dg_sem.at[i % RING])
+
+    saved_copy = pltpu.make_async_copy(xs_ref.at[layer], xs_s, xs_sem)
+
+    def enter(i):
+        @pl.when(i + RING - 1 < n_tiles)
+        def _():
+            down_copy(i + RING - 1).start()
+            slope_copy(i + RING - 1).start()
+
+        @pl.when(i + RING - 2 < n_tiles)
+        def _():
+            up_copy(i + RING - 2).start()
+
+        @pl.when(i + 1 < n_tiles)
+        def _():
+            down_copy(i + 1).wait()
+            slope_copy(i + 1).wait()
+
+        up_copy(i).wait()
+
+    def hidden_half(i, r):
+        d_hidden = dot_nt(c_ref[r, :], wd_s[i % RING]).astype(BF16).astype(F32)
+        du_s[r, :] = (d_hidden * dg_s[i % RING, r, :]).astype(BF16)
+
+    for i in range(min(RING - 1, n_tiles)):
+        down_copy(i).start()
+        slope_copy(i).start()
+        if i < RING - 2:
+            up_copy(i).start()
+    saved_copy.start()
+    down_copy(0).wait()
+    slope_copy(0).wait()
+    enter(0)
+    for r in chunks:
+        d_mixed = dot_nt(c_ref[r, :], wp_ref[0]).astype(BF16).astype(F32)
+        gate_act, slope = gelu_pair(gp_ref[0, r, :])
+        gr_ref[r, :] = gate_act * d_mixed
+        d_gate = (slope * (d_mixed * e_ref[0, r, :].astype(F32))).astype(BF16)
+        dng_s[r, :] = dot_nt(d_gate, wg_ref[0]).astype(BF16)
+        acc_s[r, :] = jnp.zeros((r.size, acc_s.shape[1]), F32)
+        hidden_half(0, r)
+
+    def tile_step(i, carry):
+        enter(i)
         for r in chunks:
-            d_mixed = dot_nt(c_ref[r, :], wp_ref[0]).astype(BF16).astype(F32)
-            gate_act, slope = gelu_pair(gp_ref[0, r, :])
-            gr_ref[r, :] = gate_act * d_mixed
-            d_gate = (slope * (d_mixed * e_ref[0, r, :].astype(F32))).astype(BF16)
-            dng_s[r, :] = dot_nt(d_gate, wg_ref[0]).astype(BF16)
-            acc_s[r, :] = jnp.zeros((r.size, acc_s.shape[1]), F32)
-            hidden_half(r)
-
-    @pl.when((tile > 0) & (tile < n_tiles))
-    def _():
-        for r in chunks:
-            acc_s[r, :] += dot_nt(du_s[r, :], wu_ref[0])
-            hidden_half(r)
-
-    @pl.when(tile == n_tiles)
-    def _():
-        for r in chunks:
-            acc = acc_s[r, :] + dot_nt(du_s[r, :], wu_ref[0])
-            d_n = (acc.astype(BF16).astype(F32) + dng_s[r, :].astype(F32)).astype(BF16).astype(F32)
-            x_f = xs_ref[0, r, :].astype(F32)
-            inv = lax.rsqrt(jnp.mean(x_f * x_f, axis=-1, keepdims=True) + NORM_EPS)
-            proj = jnp.mean(d_n * x_f, axis=-1, keepdims=True)
-            d_x = d_n * inv - x_f * (inv * inv * inv * proj)
-            cot_ref[r, :] = (c_ref[r, :].astype(F32) + d_x).astype(BF16)
+            acc_s[r, :] += dot_nt(du_s[r, :], wu_s[(i - 1) % RING])
+            hidden_half(i, r)
+        return carry
+
+    lax.fori_loop(1, n_tiles, tile_step, 0)
+    saved_copy.wait()
+    for r in row_chunks(c_ref.shape[0], FWD_CHUNK):
+        acc = acc_s[r, :] + dot_nt(du_s[r, :], wu_s[(n_tiles - 1) % RING])
+        d_n = (acc.astype(BF16).astype(F32) + dng_s[r, :].astype(F32)).astype(BF16).astype(F32)
+        x_f = xs_s[r, :].astype(F32)
+        inv = lax.rsqrt(jnp.mean(x_f * x_f, axis=-1, keepdims=True) + NORM_EPS)
+        proj = jnp.mean(d_n * x_f, axis=-1, keepdims=True)
+        d_x = d_n * inv - x_f * (inv * inv * inv * proj)
+        cot_ref[r, :] = (c_ref[r, :].astype(F32) + d_x).astype(BF16)
 
 
 def run_backward(layer, cot, xs, fetched, gp, dg, w_up, w_down, w_gate, w_proj):
@@ -166,24 +246,27 @@
     rows, e_dim = cot.shape[0], w_gate.shape[2]
     n_tiles = ffn // F_TILE
     whole = lambda *s: pl.BlockSpec(s, lambda j: (0, 0))
+    in_hbm = pl.BlockSpec(memory_space=pl.ANY)
     at_layer = lambda *s: pl.BlockSpec((1,) + s, lambda j: (layer, 0, 0))
     return pl.pallas_call(
-        functools.partial(backward_body, n_tiles),
-        grid=(n_tiles + 1,),
-        in_specs=[
-            whole(rows, d_model),
-            at_layer(rows, d_model),
-            at_layer(rows, e_dim),
-            at_layer(rows, e_dim),
-            pl.BlockSpec((1, 1, rows, F_TILE), lambda j: (layer, jnp.minimum(j, n_tiles - 1), 0, 0)),
-            pl.BlockSpec((1, d_model, F_TILE), lambda j: (layer, 0, jnp.maximum(j - 1, 0))),
-            pl.BlockSpec((1, F_TILE, d_model), lambda j: (layer, jnp.minimum(j, n_tiles - 1), 0)),
-            at_layer(d_model, e_dim),
-            at_layer(e_dim, d_model),
-        ],
+        functools.partial(backward_body, layer, n_tiles),
+        grid=(1,),
+        in_specs=[whole(rows, d_model), in_hbm, at_layer(rows, e_dim), at_layer(rows, e_dim), in_hbm, in_hbm, in_hbm, at_layer(d_model, e_dim), at_layer(e_dim, d_model)],
         out_specs=[whole(rows, d_model), whole(rows, e_dim)],
         out_shape=[jax.ShapeDtypeStruct((rows, d_model), BF16), jax.ShapeDtypeStruct((rows, e_dim), F32)],
-        scratch_shapes=[pltpu.VMEM((rows, d_model), BF16), pltpu.VMEM((rows, F_TILE), BF16), pltpu.VMEM((rows, d_model), F32)],
+        scratch_shapes=[
+            pltpu.VMEM((rows, d_model), BF16),
+            pltpu.VMEM((rows, d_model), BF16),
+            pltpu.VMEM((rows, F_TILE), BF16),
+            pltpu.VMEM((rows, d_model), F32),
+            pltpu.VMEM((RING, d_model, F_TILE), BF16),
+            pltpu.VMEM((RING, F_TILE, d_model), BF16),
+            pltpu.VMEM((RING, rows, F_TILE), F32),
+            pltpu.SemaphoreType.DMA((RING,)),
+            pltpu.SemaphoreType.DMA((RING,)),
+            pltpu.SemaphoreType.DMA((RING,)),
+            pltpu.SemaphoreType.DMA,
+        ],
         cost_estimate=pl.CostEstimate(flops=4 * rows * d_model * ffn, bytes_accessed=40_000_000, transcendentals=0),
         compiler_params=pltpu.CompilerParams(dimension_semantics=('arbitrary',), vmem_limit_bytes=56 * 2**20),
         name='backward',
@@ -253,16 +336,24 @@
 
 def place_body(group, n_group, idx_bits, n_blocks, tail, starts_ref, keys_ref, *refs):
     rows_refs, out_ref, buf, sems = refs[:n_group], refs[-3], refs[-2], refs[-1]
-    block = pl.program_id(0)
-    slot = block % PLACE_BUFS
-
-    def copy(at, which, rows):
-        where = pl.ds(pl.multiple_of(at * OUT_ROWS, OUT_ROWS), rows)
+    first = (n_blocks * 3) // 4
+    tail_step = n_blocks - 1 - first
+    step = pl.program_id(0)
+    block = (step + first) % n_blocks
+    slot = step % PLACE_BUFS
+
+    def copy(at, rows):
+        where = pl.ds(pl.multiple_of(((at + first) % n_blocks) * OUT_ROWS, OUT_ROWS), rows)
+        which = at % PLACE_BUFS
         return pltpu.make_async_copy(buf.at[which, :, pl.ds(0, rows), :], out_ref.at[pl.ds(group * n_group, n_group), where, :], sems.at[which])
 
-    @pl.when(block >= PLACE_BUFS)
-    def _():
-        copy(block - PLACE_BUFS, slot, OUT_ROWS).wait()
+    @pl.when((step >= PLACE_BUFS) & (step != tail_step + PLACE_BUFS))
+    def _():
+        copy(step - PLACE_BUFS, OUT_ROWS).wait()
+
+    @pl.when(step == tail_step + PLACE_BUFS)
+    def _():
+        copy(step - PLACE_BUFS, tail).wait()
 
     buf[slot] = jnp.zeros(buf.shape[1:], F32)
     start, end = starts_ref[block], starts_ref[block + 1]
@@ -285,15 +376,18 @@
     zero = jnp.zeros((1, buf.shape[3]), F32)
     lax.fori_loop(0, (end - start + PLACE_UNROLL - 1) // PLACE_UNROLL, go, (jnp.int32(-1),) + (zero,) * n_group)
 
-    @pl.when(block < n_blocks - 1)
-    def _():
-        copy(block, slot, OUT_ROWS).start()
-
-    @pl.when(block == n_blocks - 1)
-    def _():
-        copy(block, slot, tail).start()
+    @pl.when(step != tail_step)
+    def _():
+        copy(step, OUT_ROWS).start()
+
+    @pl.when(step == tail_step)
+    def _():
+        copy(step, tail).start()
+
+    @pl.when(step == n_blocks - 1)
+    def _():
         for at in range(max(0, n_blocks - PLACE_BUFS), n_blocks):
-            copy(at, at % PLACE_BUFS, tail if at == n_blocks - 1 else OUT_ROWS).wait()
+            copy(at, tail if at == tail_step else OUT_ROWS).wait()
 
 
 def run_place(group, starts, keys, rows_list, d_tables, shape):

time: 617 us -> 593 us (0.961)
  Pallas kernels: 565 us -> 540 us
    pallas_call x2, Pallas kernels: 118 us -> 107 us  [run_place(): pl.pallas_call(functools.partial(place_body, group, n_group, idx_bits, n_...]
    pallas_call x1, Pallas kernels: 206 us -> 198 us  [run_forward(): pl.pallas_call(functools.partial(forward_body, n_layers, n_tiles), grid=(...]
  transfers between devices with their start and end apart: 8 -> 8, of which waited for: 1 -> 1; matrix products, arithmetic and copies ran while one was open for 1% -> 2% of each run, Pallas kernels for 38% -> 38%
where the time goes in v4:
time: 593 us; the launch traced here: 586 us
  Pallas kernels  540 us (91%)
  between operations  14.5 us (2%)
  blocking collectives  13.1 us (2%)
  other arithmetic  12 us (2%)
    pallas_call x6, Pallas kernels, run_backward(): pl.pallas_call(functools.partial(backward_body, layer, n_tiles), grid=(1,...  203 us
    pallas_call x1, Pallas kernels, run_forward(): pl.pallas_call(functools.partial(forward_body, n_layers, n_tiles), grid=(...  198 us
    pallas_call x2, Pallas kernels, run_place(): pl.pallas_call(functools.partial(place_body, group, n_group, idx_bits, n_...  107 us
    pallas_call x1, Pallas kernels, run_fetch(): pl.pallas_call(functools.partial(fetch_body, n_layers, FETCH_TOK, n_steps...  32.7 us
    all_gather x1, blocking collectives, device_body(): all_ids = lax.all_gather(tok_ids, ('dp', 'emb'), axis=0, tiled=True)  13.1 us
  transfers between devices with their start and end apart: 8, of which 1 were waited for; matrix products, arithmetic and copies ran while one was open for 2% of the time, Pallas kernels for 38%

profile of v4, /device:TPU:0, one launch (start us, length us, event | category | flops | bytes accessed | tf_op | source)
XLA Modules:
  0.0 585.8 jit_solution(9805862914767976329)
XLA Ops:
  7.2 0.0 all-gather.7.cloned.1.call-start
  7.2 0.9 collective-permute-start
  8.1 0.7 compare_and_fusion
  8.8 0.1 collective-permute-done
  8.9 0.6 fusion.off_ref
  9.5 0.0 copy-start.1
  9.5 32.7 %fetch_rows.1 = bf16[6,2048,128]{2,1,0:T(8,128)(2,1)} custom-call(s32[2048]{0:T(1024)} %fusion.off_ref, bf16[6,75968,128]{2,1,0:T(8,128)(2,1)} %table_ref.1), custom_call_target="tpu_custom_call" | custom-call | flops 2000000000 | bytes 30000000 | tf_op jit(solution)/shard_map/fetch_rows/pallas_call | solution.py:321
  42.2 0.0 copy-start
  42.2 2.8 slice.9
  45.1 0.3 collective-permute-start.1
  45.4 0.0 copy-done.1
  45.4 13.1 %all_gather.21 = s32[8192]{0:T(1024)S(1)} all-gather(s32[1024]{0:T(1024)S(1)} %copy-done.1), channel_id=1, replica_groups=mesh['dp'=4,'emb'=2] {'dp','emb'}, dimensions={0}, use_global_device_ids=true | all-gather | bytes 36864 | tf_op jit(solution)/shard_map/all_gather | solution.py:446
  58.5 6.8 %sort.15 = (s32[8192]{0:T(1024)S(1)}, s32[8192]{0:T(1024)}) sort(s32[8192]{0:T(1024)S(1)} %get-tuple-element.63, s32[8192]{0:T(1024)S(1)} %iota.15), dimensions={0}, to_apply=%region_0.1 | sort | flops 106496 | bytes 131072 | tf_op jit(solution)/shard_map/jit(sort)/sort | solution.py:451
  65.3 0.6 concatenate.6.keys_ref
  65.9 1.0 convert_reduce_fusion.starts_ref
  67.0 0.0 collective-permute-done.1
  67.0 0.0 copy-done
  67.0 2.8 slice_select_fusion.e_ref
  69.8 198.0 %forward.1 = (bf16[1024,896]{1,0:T(8,128)(2,1)}, bf16[6,1024,896]{2,1,0:T(8,128)(2,1)}, f32[6,19,1024,256]{3,2,1,0:T(8,128)}, f32[6,1024,128]{2,1,0:T(8,128)}) custom-call(bf16[1024,896]{1,0:T(8,128)(2,1)} %x_ref.1, bf16[6,1024,128]{2,1,0:T(8,128)(2,1)} %slice_select_fusion.e_ref, bf16[6,896,4864]{2,1,0:T(8,128)(2,1)} %wu_ref.13, ...), custom_call_target="tpu_custom_call" | custom-call | flops 107105746944 | bytes 240000000 | tf_op jit(solution)/shard_map/forward/pallas_call | solution.py:143
  267.8 33.7 %backward.6 = (bf16[1024,896]{1,0:T(8,128)(2,1)}, f32[1024,128]{1,0:T(8,128)}) custom-call(bf16[1024,896]{1,0:T(8,128)(2,1)} %c_ref.1, bf16[6,1024,896]{2,1,0:T(8,128)(2,1)} %get-tuple-element.37.xs_ref, bf16[6,1024,128]{2,1,0:T(8,128)(2,1)} %slice_select_fusion.e_ref, f32[6,1024,128]{2,1,0:T(8,128)} %get-tuple-element.38.gp_ref, ...), custom_call_target="tpu_custom_call" | custom-call | flops 17850957824 | bytes 40000000 | tf_op jit(solution)/shard_map/backward/pallas_call | solution.py:251
  301.5 0.0 all-gather.7.cloned.1.call-update
  301.6 0.3 all-gather.9.cloned.1.call-start
  301.8 33.8 %backward.7 = (bf16[1024,896]{1,0:T(8,128)(2,1)}, f32[1024,128]{1,0:T(8,128)}) custom-call(bf16[1024,896]{1,0:T(8,128)(2,1)} %get-tuple-element.40.c_ref, bf16[6,1024,896]{2,1,0:T(8,128)(2,1)} %get-tuple-element.37.xs_ref, bf16[6,1024,128]{2,1,0:T(8,128)(2,1)} %slice_select_fusion.e_ref, f32[6,1024,128]{2,1,0:T(8,128)} %get-tuple-element.38.gp_ref, ...), custom_call_target="tpu_custom_call" | custom-call | flops 17850957824 | bytes 40000000 | tf_op jit(solution)/shard_map/backward/pallas_call | solution.py:251
  335.6 0.0 all-gather.9.cloned.1.call-update
  335.6 0.0 all-gather.11.cloned.1.call-start
  335.7 0.0 all-gather.7.cloned.1.call-done.refs_2_
  335.7 33.9 %backward.8 = (bf16[1024,896]{1,0:T(8,128)(2,1)}, f32[1024,128]{1,0:T(8,128)}) custom-call(bf16[1024,896]{1,0:T(8,128)(2,1)} %get-tuple-element.43.c_ref, bf16[6,1024,896]{2,1,0:T(8,128)(2,1)} %get-tuple-element.37.xs_ref, bf16[6,1024,128]{2,1,0:T(8,128)(2,1)} %slice_select_fusion.e_ref, f32[6,1024,128]{2,1,0:T(8,128)} %get-tuple-element.38.gp_ref, ...), custom_call_target="tpu_custom_call" | custom-call | flops 17850957824 | bytes 40000000 | tf_op jit(solution)/shard_map/backward/pallas_call | solution.py:251
  369.6 0.0 all-gather.11.cloned.1.call-update
  369.6 0.4 all-gather.13.cloned.1.call-start
  370.0 0.0 all-gather.9.cloned.1.call-done.refs_1_
  370.1 33.8 %backward.9 = (bf16[1024,896]{1,0:T(8,128)(2,1)}, f32[1024,128]{1,0:T(8,128)}) custom-call(bf16[1024,896]{1,0:T(8,128)(2,1)} %get-tuple-element.46.c_ref, bf16[6,1024,896]{2,1,0:T(8,128)(2,1)} %get-tuple-element.37.xs_ref, bf16[6,1024,128]{2,1,0:T(8,128)(2,1)} %slice_select_fusion.e_ref, f32[6,1024,128]{2,1,0:T(8,128)} %get-tuple-element.38.gp_ref, ...), custom_call_target="tpu_custom_call" | custom-call | flops 17850957824 | bytes 40000000 | tf_op jit(solution)/shard_map/backward/pallas_call | solution.py:251
  403.9 0.0 all-gather.13.cloned.1.call-update
  403.9 0.0 all-gather.15.cloned.1.call-start
  404.0 0.0 all-gather.11.cloned.1.call-done.refs_0_
  404.0 33.8 %backward.10 = (bf16[1024,896]{1,0:T(8,128)(2,1)}, f32[1024,128]{1,0:T(8,128)}) custom-call(bf16[1024,896]{1,0:T(8,128)(2,1)} %get-tuple-element.49.c_ref, bf16[6,1024,896]{2,1,0:T(8,128)(2,1)} %get-tuple-element.37.xs_ref, bf16[6,1024,128]{2,1,0:T(8,128)(2,1)} %slice_select_fusion.e_ref, f32[6,1024,128]{2,1,0:T(8,128)} %get-tuple-element.38.gp_ref, ...), custom_call_target="tpu_custom_call" | custom-call | flops 17850957824 | bytes 40000000 | tf_op jit(solution)/shard_map/backward/pallas_call | solution.py:251
  437.7 0.0 all-gather.15.cloned.1.call-update
  437.8 0.2 all-gather.17.cloned.1.call-start
  438.0 0.0 all-gather.13.cloned.1.call-done.refs_2_
  438.0 33.7 %backward.11 = (bf16[1024,896]{1,0:T(8,128)(2,1)}, f32[1024,128]{1,0:T(8,128)}) custom-call(bf16[1024,896]{1,0:T(8,128)(2,1)} %get-tuple-element.52.c_ref, bf16[6,1024,896]{2,1,0:T(8,128)(2,1)} %get-tuple-element.37.xs_ref, bf16[6,1024,128]{2,1,0:T(8,128)(2,1)} %slice_select_fusion.e_ref, f32[6,1024,128]{2,1,0:T(8,128)} %get-tuple-element.38.gp_ref, ...), custom_call_target="tpu_custom_call" | custom-call | flops 17850957824 | bytes 40000000 | tf_op jit(solution)/shard_map/backward/pallas_call | solution.py:251
  471.8 0.0 all-gather.15.cloned.1.call-done.refs_1_
  471.8 0.0 all-gather.17.cloned.1.call-update
  471.8 53.5 %place_rows.2.refs_3_ = f32[6,75968,128]{2,1,0:T(8,128)} custom-call(s32[76]{0:T(128)} %convert_reduce_fusion.starts_ref, s32[8200]{0:T(1024)} %concatenate.6.keys_ref, f32[8192,128]{1,0:T(8,128)} %all-gather.11.cloned.1.call-done.refs_0_, f32[8192,128]{1,0:T(8,128)} %all-gather.9.cloned.1.call-done.refs_1_, f32[8192,128]{1,0:T(8,128)} %all-gather.7.cloned.1.call-done.refs_2_), custom_call_target="tpu_custom_call" | custom-call | flops 30000001024 | bytes 132000000 | tf_op jit(solution)/shard_map/place_rows/pallas_call | solution.py:406
  525.3 0.0 all-gather.17.cloned.1.call-done.refs_0_
  525.3 53.5 %place_rows.3 = f32[6,75968,128]{2,1,0:T(8,128)} custom-call(s32[76]{0:T(128)} %convert_reduce_fusion.starts_ref, s32[8200]{0:T(1024)} %concatenate.6.keys_ref, f32[8192,128]{1,0:T(8,128)} %all-gather.17.cloned.1.call-done.refs_0_, f32[8192,128]{1,0:T(8,128)} %all-gather.15.cloned.1.call-done.refs_1_, ...), custom_call_target="tpu_custom_call", output_to_operand_aliasing={{}: (5, {})} | custom-call | flops 30000001024 | bytes 132000000 | tf_op jit(solution)/shard_map/place_rows/pallas_call | solution.py:406
  (4 shorter events, 0.0 us)
Async XLA Ops:
  7.2 328.5 %all-gather.7.cloned.1.call-start = ((), (), s32[]{:S(2)}) async-start(), calls=%async_computation | async-start | bytes 4718592 | tf_op jit(solution)/shard_map/all_gather | solution.py:470
  7.2 1.7 collective-permute-start
  9.5 35.9 %copy-start.1 = (s32[1024]{0:T(1024)S(1)}, s32[1024]{0:T(1024)}, u32[]{:S(2)}) copy-start(s32[1024]{0:T(1024)} %param.8) | copy-start | bytes 12292
  42.2 24.7 %copy-start = (bf16[6,2048,128]{2,1,0:T(8,128)(2,1)S(1)}, bf16[6,2048,128]{2,1,0:T(8,128)(2,1)}, u32[]{:S(2)}) copy-start(bf16[6,2048,128]{2,1,0:T(8,128)(2,1)} %fetch_rows.1) | copy-start | bytes 9437188
  45.1 21.9 %collective-permute-start.1 = (bf16[6,1024,128]{2,1,0:T(8,128)(2,1)}, bf16[6,1024,128]{2,1,0:T(8,128)(2,1)}, u32[]{:S(2)}, u32[]{:S(2)}) collective-permute-start(bf16[6,1024,128]{2,1,0:T(8,128)(2,1)} %slice.9), channel_id=1, source_target_pairs={{0,1},{1,0},{2,3},{3,2},{4,5},{5,4},{6,7},{7,6}} | collective-permute-start | bytes 4718600 | tf_op jit(solution)/shard_map/ppermute | solution.py:443
  301.6 68.5 %all-gather.9.cloned.1.call-start = ((), (), s32[]{:S(2)}) async-start(), calls=%async_computation.1 | async-start | bytes 4718592 | tf_op jit(solution)/shard_map/all_gather | solution.py:470
  335.6 68.4 %all-gather.11.cloned.1.call-start = ((), (), s32[]{:S(2)}) async-start(), calls=%async_computation.2 | async-start | bytes 4718592 | tf_op jit(solution)/shard_map/all_gather | solution.py:470
  369.6 68.4 %all-gather.13.cloned.1.call-start = ((), (), s32[]{:S(2)}) async-start(), calls=%async_computation.3 | async-start | bytes 4718592 | tf_op jit(solution)/shard_map/all_gather | solution.py:470
  403.9 67.9 %all-gather.15.cloned.1.call-start = ((), (), s32[]{:S(2)}) async-start(), calls=%async_computation.4 | async-start | bytes 4718592 | tf_op jit(solution)/shard_map/all_gather | solution.py:470
  437.8 87.5 %all-gather.17.cloned.1.call-start = ((), (), s32[]{:S(2)}) async-start(), calls=%async_computation.5 | async-start | bytes 4718592 | tf_op jit(solution)/shard_map/all_gather | solution.py:470
Sparse Core Ops, SparseCore 0:
  301.7 30.7 all-gather.6
  335.7 30.7 all-gather.8
  369.7 30.7 all-gather.10
  404.0 30.7 all-gather.12
  437.9 30.7 all-gather.14
  471.9 30.7 all-gather.16

commit v5 on v4

--- a/solution.py
+++ b/solution.py
@@ -11,7 +11,7 @@
 GELU_K = 0.7978845608028654
 GELU_A = 0.044715
 F_TILE = 256
-RING = 6
+RING = 8
 SLOPE_RING = 4
 FWD_CHUNK = 256
 BWD_CHUNK = 1024
@@ -46,7 +46,7 @@
 def weight_copy(src, buf, sems, layer, tile, index, by_rows):
     span = pl.ds(pl.multiple_of(tile * F_TILE, F_TILE), F_TILE)
     part = src.at[layer, span, :] if by_rows else src.at[layer, :, span]
-    slot = index % RING
+    slot = index & (RING - 1)
     return pltpu.make_async_copy(part, buf.at[slot], sems.at[slot])
 
 
@@ -63,7 +63,7 @@
         return weight_copy(wd_ref, wd_s, wd_sem, i // n_tiles, i % n_tiles, i, True)
 
     def slope_copy(i):
-        return pltpu.make_async_copy(dg_s.at[i % SLOPE_RING], dg_ref.at[i // n_tiles, i % n_tiles], dg_sem.at[i % SLOPE_RING])
+        return pltpu.make_async_copy(dg_s.at[i & (SLOPE_RING - 1)], dg_ref.at[i // n_tiles, i % n_tiles], dg_sem.at[i & (SLOPE_RING - 1)])
 
     def enter(i):
         @pl.when(i + RING - 1 < total)
@@ -85,8 +85,8 @@
             slope_copy(i - SLOPE_RING).wait()
 
     def up_half(i, r):
-        act, slope = gelu_pair(dot_nn(u_s[r, :], wu_s[i % RING]))
-        dg_s[i % SLOPE_RING, r, :] = slope
+        act, slope = gelu_pair(dot_nn(u_s[r, :], wu_s[i & (RING - 1)]))
+        dg_s[i & (SLOPE_RING - 1), r, :] = slope
         h_s[r, :] = act.astype(BF16)
 
     @pl.when(layer == 0)
@@ -117,14 +117,14 @@
         i = first + tile
         enter(i)
         for r in chunks:
-            acc_s[r, :] += dot_nn(h_s[r, :], wd_s[(i - 1) % RING])
+            acc_s[r, :] += dot_nn(h_s[r, :], wd_s[(i - 1) & (RING - 1)])
             up_half(i, r)
         slope_copy(i).start()
         return carry
 
     lax.fori_loop(1, n_tiles, tile_step, 0)
     for r in chunks:
-        x_s[r, :] = (acc_s[r, :] + dot_nn(h_s[r, :], wd_s[(first + n_tiles - 1) % RING])).astype(BF16)
+        x_s[r, :] = (acc_s[r, :] + dot_nn(h_s[r, :], wd_s[(first + n_tiles - 1) & (RING - 1)])).astype(BF16)
 
     @pl.when(layer == n_layers - 1)
     def _():
@@ -179,7 +179,7 @@
         return weight_copy(wd_ref, wd_s, wd_sem, layer, i, i, True)
 
     def slope_copy(i):
-        return pltpu.make_async_copy(dg_ref.at[layer, i], dg_s.at[i % RING], dg_sem.at[i % RING])
+        return pltpu.make_async_copy(dg_ref.at[layer, i], dg_s.at[i & (RING - 1)], dg_sem.at[i & (RING - 1)])
 
     saved_copy = pltpu.make_async_copy(xs_ref.at[layer], xs_s, xs_sem)
 
@@ -201,8 +201,8 @@
         up_copy(i).wait()
 
     def hidden_half(i, r):
-        d_hidden = dot_nt(c_ref[r, :], wd_s[i % RING]).astype(BF16).astype(F32)
-        du_s[r, :] = (d_hidden * dg_s[i % RING, r, :]).astype(BF16)
+        d_hidden = dot_nt(c_ref[r, :], wd_s[i & (RING - 1)]).astype(BF16).astype(F32)
+        du_s[r, :] = (d_hidden * dg_s[i & (RING - 1), r, :]).astype(BF16)
 
     for i in range(min(RING - 1, n_tiles)):
         down_copy(i).start()
@@ -225,7 +225,7 @@
     def tile_step(i, carry):
         enter(i)
         for r in chunks:
-            acc_s[r, :] += dot_nt(du_s[r, :], wu_s[(i - 1) % RING])
+            acc_s[r, :] += dot_nt(du_s[r, :], wu_s[(i - 1) & (RING - 1)])
             hidden_half(i, r)
         return carry
 
@@ -280,7 +280,7 @@
         def go(i, carry):
             for k in range(8):
                 tok = i * 8 + k
-                tile = off_ref[at * n_tok + tok] // 8
+                tile = off_ref[at * n_tok + tok] >> 3
                 pltpu.make_async_copy(table_ref.at[:, pl.ds(pl.multiple_of(tile * 8, 8), 8), :], buf.at[slot, tok], sems.at[slot]).start(priority=k % 2)
             return carry
 
@@ -303,7 +303,7 @@
         for half in range(2):
             for k in range(8):
                 tok = i * 16 + half * 8 + k
-                shift = (k + 8 - off_ref[step * n_tok + tok] % 8) % 8
+                shift = (k - off_ref[step * n_tok + tok]) & 7
                 for l in range(n_layers):
                     moved = pltpu.roll(buf[slot, tok, l].astype(F32), shift, axis=0)
                     halves[l][half] = moved if k == 0 else jnp.where(sub == k, moved, halves[l][half])
@@ -421,7 +421,7 @@
 
 
 def solution(mesh):
-    n_emb = mesh.shape['emb']
+    n_emb, n_dp = mesh.shape['emb'], mesh.shape['dp']
     tok_spec = P(('dp', 'emb'))
     act_spec = P(('dp', 'emb'), None)
     table_spec = P(None, 'emb', None)
@@ -443,12 +443,20 @@
         from_peer = lax.ppermute(served[:, tok_count:], 'emb', swap)
         fetched = jnp.where(own_mask[None, :, None], served[:, :tok_count], from_peer)
 
-        all_ids = lax.all_gather(tok_ids, ('dp', 'emb'), axis=0, tiled=True)
+        all_ids = jnp.concatenate([tok_ids, peer_ids])
+        dp_at = lax.axis_index('dp')
+        emb_at = lax.axis_index('emb')
+        owners = dp_at * n_emb + jnp.array([0, 1]) * (1 - 2 * emb_at) + emb_at
+        for step in (1, 2):
+            hop = [(i, i ^ step) for i in range(n_dp)]
+            all_ids = jnp.concatenate([all_ids, lax.ppermute(all_ids, 'dp', hop)])
+        owners = jnp.concatenate([owners + ((dp_at ^ far) - dp_at) * n_emb for far in range(n_dp)])
         n_all = all_ids.shape[0]
         idx_bits = (n_all - 1).bit_length()
+        token_at = (owners[:, None] * tok_count + jnp.arange(tok_count, dtype=jnp.int32)[None, :]).reshape(-1).astype(jnp.int32)
         all_off = all_ids - base
         all_off = jnp.where((all_off >= 0) & (all_off < range_rows), all_off, range_rows)
-        keys = jnp.sort((all_off << idx_bits) | jnp.arange(n_all, dtype=jnp.int32))
+        keys = jnp.sort((all_off << idx_bits) | token_at)
         n_blocks = pl.cdiv(range_rows, OUT_ROWS)
         pad = jnp.full((PLACE_UNROLL,), range_rows << idx_bits, jnp.int32)
         bounds = jnp.minimum(jnp.arange(n_blocks + 1, dtype=jnp.int32) * OUT_ROWS, range_rows)

time: 593 us -> 580 us (0.978)
  blocking collectives: 13.1 us -> 0 us
  Pallas kernels: 540 us -> 532 us
    all_gather x1 -> x0, blocking collectives: 13.1 us -> none  [device_body(): all_ids = lax.all_gather(tok_ids, ('dp', 'emb'), axis=0, tiled=True)]
    pallas_call x1, Pallas kernels: 32.7 us -> 22.1 us  [run_fetch(): pl.pallas_call(functools.partial(fetch_body, n_layers, FETCH_TOK, n_steps...]
    pallas_call x2, Pallas kernels: 107 us -> 116 us  [run_place(): pl.pallas_call(functools.partial(place_body, group, n_group, idx_bits, n_...]
  transfers between devices with their start and end apart: 8 -> 10, of which waited for: 1 -> 3; matrix products, arithmetic and copies ran while one was open for 2% -> 2% of each run, Pallas kernels for 38% -> 39%
where the time goes in v5:
time: 580 us; the launch traced here: 571 us
  Pallas kernels  532 us (92%)
  between operations  14.7 us (3%)
  other arithmetic  12.2 us (2%)
    pallas_call x6, Pallas kernels, run_backward(): pl.pallas_call(functools.partial(backward_body, layer, n_tiles), grid=(1,...  201 us
    pallas_call x1, Pallas kernels, run_forward(): pl.pallas_call(functools.partial(forward_body, n_layers, n_tiles), grid=(...  192 us
    pallas_call x2, Pallas kernels, run_place(): pl.pallas_call(functools.partial(place_body, group, n_group, idx_bits, n_...  116 us
    pallas_call x1, Pallas kernels, run_fetch(): pl.pallas_call(functools.partial(fetch_body, n_layers, FETCH_TOK, n_steps...  22.1 us
  transfers between devices with their start and end apart: 10, of which 3 were waited for; matrix products, arithmetic and copies ran while one was open for 2% of the time, Pallas kernels for 39%

profile of v5, /device:TPU:0, one launch (start us, length us, event | category | flops | bytes accessed | tf_op | source)
XLA Modules:
  0.0 571.4 jit_solution(4184242847430910074)
XLA Ops:
  7.2 0.0 all-gather.7.cloned.1.call-start
  7.2 0.9 collective-permute-start
  8.1 0.7 compare_and_fusion
  8.8 0.1 collective-permute-done
  8.9 0.6 fusion.off_ref
  9.5 22.1 %fetch_rows.1 = bf16[6,2048,128]{2,1,0:T(8,128)(2,1)} custom-call(s32[2048]{0:T(1024)} %fusion.off_ref, bf16[6,75968,128]{2,1,0:T(8,128)(2,1)} %table_ref.1), custom_call_target="tpu_custom_call" | custom-call | flops 2000000000 | bytes 30000000 | tf_op jit(solution)/shard_map/fetch_rows/pallas_call | solution.py:321
  31.6 0.0 copy-start.1
  31.6 0.0 copy-start
  31.7 2.8 slice.9
  34.5 0.0 collective-permute-start.3
  34.5 0.1 add_multiply_fusion
  34.6 0.0 copy-done.1
  34.6 2.8 collective-permute-start.1
  37.3 0.1 add_bitcast_fusion
  37.4 1.6 collective-permute-done.1
  39.0 0.9 collective-permute-start.2
  39.9 2.9 collective-permute-done.2
  42.7 6.8 %sort.15 = (s32[8192]{0:T(1024)S(1)}, s32[8192]{0:T(1024)}) sort(s32[8192]{0:T(1024)S(1)} %get-tuple-element.63, s32[8192]{0:T(1024)S(1)} %iota.16), dimensions={0}, to_apply=%region_0.1 | sort | flops 106496 | bytes 131072 | tf_op jit(solution)/shard_map/jit(sort)/sort | solution.py:459
  49.5 0.6 concatenate.32.keys_ref
  50.1 1.1 convert_reduce_fusion.starts_ref
  51.2 0.0 collective-permute-done.3
  51.2 2.8 slice_select_fusion.e_ref
  54.0 192.3 %forward.1 = (bf16[1024,896]{1,0:T(8,128)(2,1)}, bf16[6,1024,896]{2,1,0:T(8,128)(2,1)}, f32[6,19,1024,256]{3,2,1,0:T(8,128)}, f32[6,1024,128]{2,1,0:T(8,128)}) custom-call(bf16[1024,896]{1,0:T(8,128)(2,1)} %x_ref.1, bf16[6,1024,128]{2,1,0:T(8,128)(2,1)} %slice_select_fusion.e_ref, bf16[6,896,4864]{2,1,0:T(8,128)(2,1)} %wu_ref.13, ...), custom_call_target="tpu_custom_call" | custom-call | flops 107105746944 | bytes 240000000 | tf_op jit(solution)/shard_map/forward/pallas_call | solution.py:143
  246.4 33.6 %backward.6 = (bf16[1024,896]{1,0:T(8,128)(2,1)}, f32[1024,128]{1,0:T(8,128)}) custom-call(bf16[1024,896]{1,0:T(8,128)(2,1)} %c_ref.1, bf16[6,1024,896]{2,1,0:T(8,128)(2,1)} %get-tuple-element.37.xs_ref, bf16[6,1024,128]{2,1,0:T(8,128)(2,1)} %slice_select_fusion.e_ref, f32[6,1024,128]{2,1,0:T(8,128)} %get-tuple-element.38.gp_ref, ...), custom_call_target="tpu_custom_call" | custom-call | flops 17850957824 | bytes 40000000 | tf_op jit(solution)/shard_map/backward/pallas_call | solution.py:251
  280.0 0.0 all-gather.7.cloned.1.call-update
  280.0 0.0 all-gather.9.cloned.1.call-start
  280.1 33.5 %backward.7 = (bf16[1024,896]{1,0:T(8,128)(2,1)}, f32[1024,128]{1,0:T(8,128)}) custom-call(bf16[1024,896]{1,0:T(8,128)(2,1)} %get-tuple-element.40.c_ref, bf16[6,1024,896]{2,1,0:T(8,128)(2,1)} %get-tuple-element.37.xs_ref, bf16[6,1024,128]{2,1,0:T(8,128)(2,1)} %slice_select_fusion.e_ref, f32[6,1024,128]{2,1,0:T(8,128)} %get-tuple-element.38.gp_ref, ...), custom_call_target="tpu_custom_call" | custom-call | flops 17850957824 | bytes 40000000 | tf_op jit(solution)/shard_map/backward/pallas_call | solution.py:251
  313.5 0.0 all-gather.9.cloned.1.call-update
  313.6 0.0 all-gather.11.cloned.1.call-start
  313.6 0.0 all-gather.7.cloned.1.call-done.refs_2_
  313.6 33.7 %backward.8 = (bf16[1024,896]{1,0:T(8,128)(2,1)}, f32[1024,128]{1,0:T(8,128)}) custom-call(bf16[1024,896]{1,0:T(8,128)(2,1)} %get-tuple-element.43.c_ref, bf16[6,1024,896]{2,1,0:T(8,128)(2,1)} %get-tuple-element.37.xs_ref, bf16[6,1024,128]{2,1,0:T(8,128)(2,1)} %slice_select_fusion.e_ref, f32[6,1024,128]{2,1,0:T(8,128)} %get-tuple-element.38.gp_ref, ...), custom_call_target="tpu_custom_call" | custom-call | flops 17850957824 | bytes 40000000 | tf_op jit(solution)/shard_map/backward/pallas_call | solution.py:251
  347.4 0.0 all-gather.11.cloned.1.call-update
  347.4 0.0 all-gather.13.cloned.1.call-start
  347.5 0.0 all-gather.9.cloned.1.call-done.refs_1_
  347.5 33.5 %backward.9 = (bf16[1024,896]{1,0:T(8,128)(2,1)}, f32[1024,128]{1,0:T(8,128)}) custom-call(bf16[1024,896]{1,0:T(8,128)(2,1)} %get-tuple-element.46.c_ref, bf16[6,1024,896]{2,1,0:T(8,128)(2,1)} %get-tuple-element.37.xs_ref, bf16[6,1024,128]{2,1,0:T(8,128)(2,1)} %slice_select_fusion.e_ref, f32[6,1024,128]{2,1,0:T(8,128)} %get-tuple-element.38.gp_ref, ...), custom_call_target="tpu_custom_call" | custom-call | flops 17850957824 | bytes 40000000 | tf_op jit(solution)/shard_map/backward/pallas_call | solution.py:251
  381.0 0.0 all-gather.13.cloned.1.call-update
  381.0 0.0 all-gather.15.cloned.1.call-start
  381.1 0.0 all-gather.11.cloned.1.call-done.refs_0_
  381.1 33.7 %backward.10 = (bf16[1024,896]{1,0:T(8,128)(2,1)}, f32[1024,128]{1,0:T(8,128)}) custom-call(bf16[1024,896]{1,0:T(8,128)(2,1)} %get-tuple-element.49.c_ref, bf16[6,1024,896]{2,1,0:T(8,128)(2,1)} %get-tuple-element.37.xs_ref, bf16[6,1024,128]{2,1,0:T(8,128)(2,1)} %slice_select_fusion.e_ref, f32[6,1024,128]{2,1,0:T(8,128)} %get-tuple-element.38.gp_ref, ...), custom_call_target="tpu_custom_call" | custom-call | flops 17850957824 | bytes 40000000 | tf_op jit(solution)/shard_map/backward/pallas_call | solution.py:251
  414.8 0.0 all-gather.15.cloned.1.call-update
  414.8 0.0 all-gather.17.cloned.1.call-start
  414.8 0.0 all-gather.13.cloned.1.call-done.refs_2_
  414.9 33.4 %backward.11 = (bf16[1024,896]{1,0:T(8,128)(2,1)}, f32[1024,128]{1,0:T(8,128)}) custom-call(bf16[1024,896]{1,0:T(8,128)(2,1)} %get-tuple-element.52.c_ref, bf16[6,1024,896]{2,1,0:T(8,128)(2,1)} %get-tuple-element.37.xs_ref, bf16[6,1024,128]{2,1,0:T(8,128)(2,1)} %slice_select_fusion.e_ref, f32[6,1024,128]{2,1,0:T(8,128)} %get-tuple-element.38.gp_ref, ...), custom_call_target="tpu_custom_call" | custom-call | flops 17850957824 | bytes 40000000 | tf_op jit(solution)/shard_map/backward/pallas_call | solution.py:251
  448.3 0.0 all-gather.15.cloned.1.call-done.refs_1_
  448.3 0.0 all-gather.17.cloned.1.call-update
  448.4 57.9 %place_rows.2.refs_3_ = f32[6,75968,128]{2,1,0:T(8,128)} custom-call(s32[76]{0:T(128)} %convert_reduce_fusion.starts_ref, s32[8200]{0:T(1024)} %concatenate.32.keys_ref, f32[8192,128]{1,0:T(8,128)} %all-gather.11.cloned.1.call-done.refs_0_, f32[8192,128]{1,0:T(8,128)} %all-gather.9.cloned.1.call-done.refs_1_, f32[8192,128]{1,0:T(8,128)} %all-gather.7.cloned.1.call-done.refs_2_), custom_call_target="tpu_custom_call" | custom-call | flops 30000001024 | bytes 132000000 | tf_op jit(solution)/shard_map/place_rows/pallas_call | solution.py:406
  506.2 0.0 all-gather.17.cloned.1.call-done.refs_0_
  506.3 57.9 %place_rows.3 = f32[6,75968,128]{2,1,0:T(8,128)} custom-call(s32[76]{0:T(128)} %convert_reduce_fusion.starts_ref, s32[8200]{0:T(1024)} %concatenate.32.keys_ref, f32[8192,128]{1,0:T(8,128)} %all-gather.17.cloned.1.call-done.refs_0_, f32[8192,128]{1,0:T(8,128)} %all-gather.15.cloned.1.call-done.refs_1_, ...), custom_call_target="tpu_custom_call", output_to_operand_aliasing={{}: (5, {})} | custom-call | flops 30000001024 | bytes 132000000 | tf_op jit(solution)/shard_map/place_rows/pallas_call | solution.py:406
  (9 shorter events, 0.0 us)
Async XLA Ops:
  7.2 306.5 %all-gather.7.cloned.1.call-start = ((), (), s32[]{:S(2)}) async-start(), calls=%async_computation | async-start | bytes 4718592 | tf_op jit(solution)/shard_map/all_gather | solution.py:478
  7.2 1.7 collective-permute-start
  31.6 2.9 copy-start.1
  31.6 19.6 %copy-start = (bf16[6,2048,128]{2,1,0:T(8,128)(2,1)S(1)}, bf16[6,2048,128]{2,1,0:T(8,128)(2,1)}, u32[]{:S(2)}) copy-start(bf16[6,2048,128]{2,1,0:T(8,128)(2,1)} %fetch_rows.1) | copy-start | bytes 9437188
  34.5 16.8 %collective-permute-start.3 = (bf16[6,1024,128]{2,1,0:T(8,128)(2,1)}, bf16[6,1024,128]{2,1,0:T(8,128)(2,1)}, u32[]{:S(2)}, u32[]{:S(2)}) collective-permute-start(bf16[6,1024,128]{2,1,0:T(8,128)(2,1)} %slice.9), channel_id=1, source_target_pairs={{0,1},{1,0},{2,3},{3,2},{4,5},{5,4},{6,7},{7,6}} | collective-permute-start | bytes 4718600 | tf_op jit(solution)/shard_map/ppermute | solution.py:443
  34.6 4.4 collective-permute-start.1
  39.0 3.7 collective-permute-start.2
  280.0 67.5 %all-gather.9.cloned.1.call-start = ((), (), s32[]{:S(2)}) async-start(), calls=%async_computation.1 | async-start | bytes 4718592 | tf_op jit(solution)/shard_map/all_gather | solution.py:478
  313.6 67.5 %all-gather.11.cloned.1.call-start = ((), (), s32[]{:S(2)}) async-start(), calls=%async_computation.2 | async-start | bytes 4718592 | tf_op jit(solution)/shard_map/all_gather | solution.py:478
  347.4 67.5 %all-gather.13.cloned.1.call-start = ((), (), s32[]{:S(2)}) async-start(), calls=%async_computation.3 | async-start | bytes 4718592 | tf_op jit(solution)/shard_map/all_gather | solution.py:478
  381.0 67.3 %all-gather.15.cloned.1.call-start = ((), (), s32[]{:S(2)}) async-start(), calls=%async_computation.4 | async-start | bytes 4718592 | tf_op jit(solution)/shard_map/all_gather | solution.py:478
  414.8 91.5 %all-gather.17.cloned.1.call-start = ((), (), s32[]{:S(2)}) async-start(), calls=%async_computation.5 | async-start | bytes 4718592 | tf_op jit(solution)/shard_map/all_gather | solution.py:478
Sparse Core Ops, SparseCore 0:
  280.1 31.5 all-gather.6
  313.7 31.5 all-gather.8
  347.5 31.5 all-gather.10
  381.1 31.5 all-gather.12
  414.9 31.5 all-gather.14
  448.5 31.5 all-gather.16
